TPU v7x, 256 devices: a whole 4x4x8 slice. The times are simulated.
256 devices in a mesh: dp: 16 (over y, x), expert: 8 (over z), tensor: 2 (over core).
Axes of the slice: x: 4, y: 4, z: 8, core: 2. Of those that a mesh axis runs over, the one named last changes fastest.
Arguments:
- tokens: bfloat16 [2048, 4096], P(('dp', 'expert'), 'tensor'), may hold values from -6 to 6
- target: bfloat16 [2048, 4096], P(('dp', 'expert'), 'tensor'), may hold values from -4 to 4
- router: bfloat16 [4096, 8], P('tensor'), may hold values from -1 to 1
- w_gate: bfloat16 [8, 4096, 14336], P('expert', None, ('dp', 'tensor')), may hold values from -1 to 1
- w_up: bfloat16 [8, 4096, 14336], P('expert', None, ('dp', 'tensor')), may hold values from -1 to 1
- w_down: bfloat16 [8, 14336, 4096], P('expert', ('dp', 'tensor')), may hold values from -1 to 1
- expert_ids: int32 [2048, 2], P(('dp', 'expert')), may hold values from 0 to 7, as said below
- lengths: int32 [64], replicated, may hold values from 1 to 128, 2048 in all
- bench_ids: int32 [64], replicated, may hold values from 0 to 15
Outputs:
- mixed: bfloat16 [2048, 4096], P(('dp', 'expert'), 'tensor')
- bench_loss: float32 [16], replicated
- counts: int32 [16], replicated
Inputs may be any that keep to these rules, and one draw needn't show every extreme that they name: `expert_ids`: each row names two different experts; among the 16 rows of one device no expert is named by more than 8 rows; for each index of dp, one expert is named by exactly 8 rows of every device of that index. The lengths sum to 2048.
All inputs are finite; a program needn't handle non-finite values.
Results may differ from a plain program's by a relative error of at most 0.0085.
Values may be sent and summed in bfloat16 or wider, within the bound.
A program may use at most 128 MiB of HBM per device.

v0:
```python
import jax
import jax.numpy as jnp
from jax import lax
from jax.sharding import Mesh
from jax.sharding import PartitionSpec as P

D = 4096
NB = 16
CAP = 8
DP = ("dp_0", "dp_1")
DP_EXPERT = ("dp_0", "dp_1", "expert")
DP_EXPERT_TENSOR = ("dp_0", "dp_1", "expert", "tensor")
DP_TENSOR = ("dp_0", "dp_1", "tensor")


def cut_along(shard, dim, size):
    before, after = (shard.shape[:dim], shard.shape[dim + 1 :])
    return jnp.moveaxis(shard.reshape(*before, size, -1, *after), dim, 0)


def sent_and_summed(shard, axis, dim):
    pieces = cut_along(shard, dim, lax.axis_size(axis))
    arrived = lax.all_to_all(pieces, axis, split_axis=0, concat_axis=0, tiled=True)
    return arrived.sum(axis=0)


def one_axis_at_a_time(shard, axes):
    for axis in axes:
        shard = lax.psum(shard, axis)
    return shard


def per_device(tokens, target, router, w_gate, w_up, w_down, expert_ids, lengths, bench_ids):
    tensor_count = lax.axis_size("tensor")
    local_tokens = tokens.shape[0]
    experts = router.shape[1]
    half_cap = CAP // tensor_count
    slot_rows = tensor_count * experts * half_cap
    partial_value = jnp.dot(tokens, router, preferred_element_type=jnp.float32)
    logits = lax.psum(partial_value, "tensor")
    chosen = expert_ids[:, :, None] == jnp.arange(experts, dtype=jnp.int32)[None, None, :]
    picked = jnp.sum(jnp.where(chosen, logits[:, None, :], jnp.float32(0.0)), axis=2)
    gates = jnp.stack(
        [jax.nn.sigmoid(picked[:, 0] - picked[:, 1]), jax.nn.sigmoid(picked[:, 1] - picked[:, 0])],
        axis=1,
    )
    marks = chosen.reshape(local_tokens * 2, experts).astype(jnp.int32)
    before = jnp.cumsum(marks, axis=0) - marks
    slot = jnp.sum(before * marks, axis=1)
    flat_ids = expert_ids.reshape(local_tokens * 2)
    target_row = slot // half_cap * (experts * half_cap) + flat_ids * half_cap + slot % half_cap
    placing = (target_row[None, :] == jnp.arange(slot_rows, dtype=jnp.int32)[:, None]).reshape(
        slot_rows, local_tokens, 2
    )
    dispatch_map = jnp.any(placing, axis=2).astype(jnp.bfloat16)
    outgoing = jnp.dot(dispatch_map, tokens, preferred_element_type=jnp.float32).astype(
        jnp.bfloat16
    )
    outgoing = outgoing.reshape(tensor_count, experts, half_cap, tokens.shape[1])
    arrived = lax.all_to_all(outgoing, "expert", split_axis=1, concat_axis=1, tiled=True)
    whole = lax.all_gather(arrived, "tensor", axis=3, tiled=True)
    whole = whole.reshape(1, slot_rows, D)
    every_row = lax.all_gather(whole, DP, axis=0, tiled=True).reshape(-1, D)
    gate_w = w_gate[0]
    up_w = w_up[0]
    down_w = w_down[0]
    gate = jnp.dot(every_row, gate_w, preferred_element_type=jnp.float32)
    up = jnp.dot(every_row, up_w, preferred_element_type=jnp.float32)
    hidden = (jax.nn.silu(gate) * up).astype(jnp.bfloat16)
    summed = lax.psum_scatter(
        jnp.dot(hidden, down_w, preferred_element_type=jnp.float32),
        DP,
        scatter_dimension=0,
        tiled=True,
    )
    summed = sent_and_summed(summed, "tensor", 1)
    results = summed.astype(jnp.bfloat16).reshape(
        tensor_count, experts, half_cap, D // tensor_count
    )
    returned = lax.all_to_all(results, "expert", split_axis=1, concat_axis=1, tiled=True)
    weights = jnp.einsum("rtk,tk->tr", placing.astype(jnp.float32), gates)
    flat_back = returned.reshape(slot_rows, -1).astype(jnp.float32)
    mixed = jnp.dot(weights, flat_back, precision=lax.Precision.HIGHEST).astype(jnp.bfloat16)
    first_index = lax.axis_index(DP_EXPERT) * local_tokens
    position = first_index + jnp.arange(local_tokens, dtype=jnp.int32)
    ends = jnp.cumsum(lengths)
    starts = ends - lengths
    inside = ((position[:, None] >= starts[None, :]) & (position[:, None] < ends[None, :])).astype(
        jnp.float32
    )
    closing = jnp.any((position + 1)[:, None] == ends[None, :], axis=1)
    scored = jnp.where(closing, jnp.float32(0.0), jnp.float32(1.0))
    bench_table = bench_ids[:, None] == jnp.arange(NB, dtype=jnp.int32)[None, :]
    bench_of = jnp.dot(inside, bench_table.astype(jnp.float32), precision=lax.Precision.HIGHEST)
    diff = mixed.astype(jnp.float32) - target.astype(jnp.float32)
    token_part = jnp.sum(diff * diff, axis=1) / D
    local_sums = jnp.dot(scored * token_part, bench_of, precision=lax.Precision.HIGHEST)
    loss_sum = one_axis_at_a_time(local_sums, DP_EXPERT_TENSOR)
    counts = jnp.sum(jnp.where(bench_table, (lengths - 1)[:, None], 0), axis=0)
    bench_loss = loss_sum / jnp.maximum(counts, 1).astype(jnp.float32)
    return (mixed, bench_loss, counts)


def solution(mesh):
    split = Mesh(
        mesh.devices.reshape(4, 4, mesh.shape["expert"], mesh.shape["tensor"]),
        ("dp_0", "dp_1", "expert", "tensor"),
    )
    in_specs = (
        P(DP_EXPERT, "tensor"),
        P(DP_EXPERT, "tensor"),
        P("tensor", None),
        P("expert", None, DP_TENSOR),
        P("expert", None, DP_TENSOR),
        P("expert", DP_TENSOR, None),
        P(DP_EXPERT, None),
        P(),
        P(),
    )
    out_specs = (P(DP_EXPERT, "tensor"), P(), P())
    return jax.shard_map(
        per_device, mesh=split, in_specs=in_specs, out_specs=out_specs, check_vma=False
    )
```

profile of v0, /device:TPU:1, one launch (start us, length us, event | category | flops | bytes accessed | tf_op | source)
XLA Modules:
  0.0 317.1 jit_solution(9953797493856227956)
XLA Ops:
  7.2 0.8 copy.53
  8.0 0.1 eq.64
  8.1 0.1 fusion.13
  8.1 0.1 reduce_window_sum.18
  8.2 0.2 select_reduce_fusion
  8.4 0.1 reduce_sum.48
  8.5 0.1 copy.54
  8.6 0.7 fusion.22
  9.3 0.1 fusion.34
  9.4 0.3 convolution_convert_fusion
  9.6 0.1 reshape.108
  9.7 0.1 copy.58
  9.8 19.3 %all_to_all.15 = bf16[2,8,4,2048]{3,2,0,1:T(4,128)(2,1)S(1)} all-to-all(bf16[2,8,4,2048]{3,2,0,1:T(4,128)(2,1)S(1)} %copy.58), channel_id=1, replica_groups=mesh['dp_0'=4,'dp_1'=4,'expert'=8,'tensor'=2] {'expert'}, dimensions={1} | all-to-all | bytes 524288 | tf_op jit(solution)/shard_map/all_to_all | solution.py:60
  29.2 4.1 %all_gather.6 = bf16[2,8,4,4096]{3,2,0,1:T(4,128)(2,1)S(1)} all-gather(bf16[2,8,4,2048]{3,2,0,1:T(4,128)(2,1)S(1)} %all_to_all.15), channel_id=1, replica_groups=mesh['dp_0'=4,'dp_1'=4,'expert'=8,'tensor'=2] {'tensor'}, dimensions={3}, use_global_device_ids=true | all-gather | bytes 786432 | tf_op jit(solution)/shard_map/all_gather | solution.py:61
  33.3 0.2 copy.59
  33.5 0.9 reshape.109
  34.4 0.0 reduce-scatter.2.cloned.1.call-start
  34.5 71.8 %all-gather.2.cloned.1.call-done = bf16[16,64,4096]{2,1,0:T(8,128)(2,1)} async-done(((bf16[1,64,4096]{2,1,0:T(8,128)(2,1)}), bf16[16,64,4096]{2,1,0:T(8,128)(2,1)}) %all-gather.2.cloned.1.call-update) | async-done | bytes 8388624 | tf_op jit(solution)/shard_map/all_gather | solution.py:63
  106.3 7.5 %fusion.4 = f32[1024,448]{0,1:T(8,128)S(1)} fusion(bf16[1024,4096]{1,0:T(8,128)(2,1)} %bitcast.45, bf16[1,4096,448]{1,2,0:T(8,128)(2,1)} %param.12), kind=kOutput, calls=%fused_computation.4 | convolution fusion | flops 3758096384 | bytes 13893632 | tf_op jit(solution)/shard_map/dot_general | solution.py:67
  113.8 16.5 %fusion = f32[1024,4096]{1,0:T(8,128)} fusion(bf16[1,448,4096]{2,1,0:T(8,128)(2,1)} %param.14, f32[1024,448]{0,1:T(8,128)S(1)} %fusion.4, bf16[1024,4096]{1,0:T(8,128)(2,1)} %bitcast.46, bf16[1,4096,448]{1,2,0:T(8,128)(2,1)} %param.13), kind=kOutput, calls=%fused_computation | convolution fusion | flops 7518945280 | bytes 34340864 | tf_op jit(solution)/shard_map/dot_general | solution.py:71
  130.4 0.6 copy-done.4
  131.0 0.1 copy.63
  131.1 0.1 reduce-window.8
  131.2 0.1 reduce
  131.3 0.1 fusion.35
  131.4 3.0 psum.35
  134.4 0.1 select_reduce_fusion.1
  134.5 0.2 compare_reduce_fusion
  134.7 111.3 %reduce-scatter.2.cloned.1.call-done = f32[64,4096]{1,0:T(8,128)} async-done(((f32[1024,4096]{1,0:T(8,128)}), f32[64,4096]{1,0:T(8,128)}) %reduce-scatter.2.cloned.1.call-update) | async-done | bytes 1048592 | tf_op jit(solution)/shard_map/reduce_scatter | solution.py:70
  246.0 1.3 copy.71
  247.3 5.1 %all_to_all.16 = f32[2,64,2048]{2,1,0:T(8,128)S(1)} all-to-all(f32[2,64,2048]{2,1,0:T(8,128)S(1)} %bitcast.41), channel_id=1, replica_groups=mesh['dp_0'=4,'dp_1'=4,'expert'=8,'tensor'=2] {'tensor'}, dimensions={0} | all-to-all | bytes 2097152 | tf_op jit(solution)/shard_map/all_to_all | solution.py:23
  252.4 0.1 reduce_sum.50
  252.5 0.1 convert_element_type.37
  252.6 0.8 copy.61
  253.4 6.8 %all-to-all-start.2 = ((bf16[2,8,4,2048]{3,2,0,1:T(4,128)(2,1)}), bf16[2,8,4,2048]{3,2,0,1:T(4,128)(2,1)S(1)}, u32[]{:S(2)}, u32[]{:S(2)}) async-start(bf16[2,8,4,2048]{3,2,0,1:T(4,128)(2,1)} %copy.61), calls=%async_computation.3 | async-start | bytes 524288 | tf_op jit(solution)/shard_map/all_to_all | solution.py:80
  260.2 0.1 copy.65
  260.3 0.2 fusion.14
  260.5 0.1 fusion.11
  260.6 10.7 %all-to-all-done.2 = bf16[2,8,4,2048]{3,2,0,1:T(4,128)(2,1)S(1)} async-done(((bf16[2,8,4,2048]{3,2,0,1:T(4,128)(2,1)}), bf16[2,8,4,2048]{3,2,0,1:T(4,128)(2,1)S(1)}, u32[]{:S(2)}, u32[]{:S(2)}) %all-to-all-start.2) | async-done | bytes 262176 | tf_op jit(solution)/shard_map/all_to_all | solution.py:80
  271.3 0.1 copy.62
  271.4 0.1 reshape.112
  271.5 1.0 multiply_reduce_fusion
  272.4 0.1 convolution_bitcast_fusion
  272.6 8.0 %psum.36 = f32[16]{0:T(128)S(1)} all-reduce(f32[16]{0:T(128)S(1)} %convolution_bitcast_fusion), channel_id=1, replica_groups=mesh['dp_0'=4,'dp_1'=4,'expert'=8,'tensor'=2] {'dp_0'}, use_global_device_ids=true, to_apply=%region_10.11 | all-reduce | flops 16 | bytes 128 | tf_op jit(solution)/shard_map/psum | solution.py:29
  280.5 6.7 %psum.37 = f32[16]{0:T(128)S(1)} all-reduce(f32[16]{0:T(128)S(1)} %psum.36), channel_id=1, replica_groups=mesh['dp_0'=4,'dp_1'=4,'expert'=8,'tensor'=2] {'dp_1'}, use_global_device_ids=true, to_apply=%region_11.12 | all-reduce | flops 16 | bytes 128 | tf_op jit(solution)/shard_map/psum | solution.py:29
  287.2 10.7 %psum.38 = f32[16]{0:T(128)S(1)} all-reduce(f32[16]{0:T(128)S(1)} %psum.37), channel_id=1, replica_groups=mesh['dp_0'=4,'dp_1'=4,'expert'=8,'tensor'=2] {'expert'}, use_global_device_ids=true, to_apply=%region_12.13 | all-reduce | flops 16 | bytes 128 | tf_op jit(solution)/shard_map/psum | solution.py:29
  297.9 11.9 %psum.39 = f32[16]{0:T(128)S(1)} all-reduce(f32[16]{0:T(128)S(1)} %psum.38), channel_id=1, replica_groups=mesh['dp_0'=4,'dp_1'=4,'expert'=8,'tensor'=2] {'tensor'}, use_global_device_ids=true, to_apply=%region_13.14 | all-reduce | flops 16 | bytes 128 | tf_op jit(solution)/shard_map/psum | solution.py:29
  309.8 0.5 convert_divide_fusion
  (21 shorter events, 0.2 us)
Async XLA Ops:
  7.2 2.2 copy-start
  7.2 99.1 %all-gather.2.cloned.1.call-start = ((), (), s32[]{:S(2)}) async-start(), calls=%async_computation.4 | async-start | bytes 8912896 | tf_op jit(solution)/shard_map/all_gather | solution.py:63
  34.4 211.6 %reduce-scatter.2.cloned.1.call-start = ((), (), s32[]{:S(2)}) async-start(), calls=%async_computation.5 | async-start | bytes 17825792 | tf_op jit(solution)/shard_map/reduce_scatter | solution.py:70
  130.3 0.7 copy-start.4
  130.3 1.0 copy-start.2
  130.3 4.1 %copy-start.5 = (s32[64]{0:T(128)S(1)}, s32[64]{0:T(128)}, u32[]{:S(2)}) copy-start(s32[64]{0:T(128)} %param.17) | copy-start | bytes 772
  130.3 4.2 %copy-start.3 = (s32[16,2]{0,1:T(2,128)S(1)}, s32[16,2]{0,1:T(2,128)}, u32[]{:S(2)}) copy-start(s32[16,2]{0,1:T(2,128)} %param.15) | copy-start | bytes 388
  134.5 175.3 %copy-start.6 = (s32[16]{0:T(128)}, s32[16]{0:T(128)S(1)}, u32[]{:S(2)}) copy-start(s32[16]{0:T(128)S(1)} %select_reduce_fusion.1) | copy-start | bytes 196
  246.0 25.5 %copy-start.1 = (bf16[16,2048]{1,0:T(8,128)(2,1)S(1)}, bf16[16,2048]{1,0:T(8,128)(2,1)}, u32[]{:S(2)}) copy-start(bf16[16,2048]{1,0:T(8,128)(2,1)} %param.10) | copy-start | bytes 196612
  253.4 17.9 %all-to-all-start.2 = ((bf16[2,8,4,2048]{3,2,0,1:T(4,128)(2,1)}), bf16[2,8,4,2048]{3,2,0,1:T(4,128)(2,1)S(1)}, u32[]{:S(2)}, u32[]{:S(2)}) async-start(bf16[2,8,4,2048]{3,2,0,1:T(4,128)(2,1)} %copy.61), calls=%async_computation.3 | async-start | bytes 524288 | tf_op jit(solution)/shard_map/all_to_all | solution.py:80
Sparse Core Ops, SparseCore 0:
  34.5 71.6 all-gather.1
  130.5 115.4 reduce-scatter.1
where the time goes:
time: 318 us; the launch traced here: 317 us
  waiting for transfers between devices  194 us (61%)
  blocking collectives  68.7 us (22%)
  matrix products  25.9 us (8%)
  between operations  14.2 us (4%)
  starting transfers between devices  6.86 us (2%)
  local copies, waits for them, and re-layouts  5.59 us (2%)
    reduce_scatter x1, waiting for transfers between devices, per_device(): lax.psum_scatter(jnp.dot(hidden, down_w, preferred_element_type=jnp.float...  111 us
    all_gather x1, waiting for transfers between devices, per_device(): every_row = lax.all_gather(whole, DP, axis=0, tiled=True).reshape(-1, D)  71.8 us
    psum x4, blocking collectives, one_axis_at_a_time(): shard = lax.psum(shard, axis)  37.2 us
    all_to_all x1, blocking collectives, per_device(): lax.all_to_all(outgoing, 'expert', split_axis=1, concat_axis=1, tiled=True)  19.3 us
    dot_general x1, matrix products, per_device(): jnp.dot(hidden, down_w, preferred_element_type=jnp.float32)  16.5 us
    all_to_all x1, waiting for transfers between devices, per_device(): lax.all_to_all(results, 'expert', split_axis=1, concat_axis=1, tiled=True)  10.7 us
    dot_general x1, matrix products, per_device(): gate = jnp.dot(every_row, gate_w, preferred_element_type=jnp.float32)  7.52 us
    all_to_all x1, starting transfers between devices, per_device(): lax.all_to_all(results, 'expert', split_axis=1, concat_axis=1, tiled=True)  6.78 us
  transfers between devices with their start and end apart: 3, of which 3 were waited for; matrix products, arithmetic and copies ran while one was open for 0% of the time, Pallas kernels for 0%

commit v1 on v0

v1 whole, which is shorter than its diff:
```python
import jax
import jax.numpy as jnp
from jax import lax
from jax.experimental import pallas as pl
from jax.experimental.pallas import tpu as pltpu
from jax.sharding import Mesh
from jax.sharding import PartitionSpec as P

D = 4096
DH = D // 2
NB = 16
CAP = 8
TOK = 16
HID = 448
NSEQ = 64
NE = 8
NQ = 2
FQ = DH // NQ
DP_EXPERT = ("dp_0", "dp_1", "expert")
DP_TENSOR = ("dp_0", "dp_1", "tensor")
MESH = pl.DeviceIdType.MESH
F32 = jnp.float32
BF16 = jnp.bfloat16
NSEMS = 62 * NQ + 40


def kernel(
    tokens, target, router, wg_hbm, wu_hbm, wd_hbm, ids, lengths, bench,
    mixed_out, loss_out, counts_out,
    OUT, ZL, XO, XP, WG, WU, WD, H, PX, PR, PO, S, R1, R2, TB, T1, T2, RET, BACK,
    LG, LGR, L1, L2, MIX, wsem, ssem, rsem,
):
    y = lax.axis_index("dp_0")
    x = lax.axis_index("dp_1")
    z = lax.axis_index("expert")
    c = lax.axis_index("tensor")

    def at(dy=0, dx=0, dz=0, dc=0):
        return {
            "dp_0": lax.rem(y + dy, 4),
            "dp_1": lax.rem(x + dx, 4),
            "expert": lax.rem(z + dz, 8),
            "tensor": lax.rem(c + dc, 2),
        }

    column = [(dz, dc) for dz in range(8) for dc in range(2)][1:]
    plane = [(dy, dx) for dy in range(4) for dx in range(4)][1:]
    barrier = pltpu.get_barrier_semaphore()
    for dz, dc in column:
        pl.semaphore_signal(barrier, inc=1, device_id=at(dz=dz, dc=dc), device_id_type=MESH)
    for dy, dx in plane:
        pl.semaphore_signal(barrier, inc=1, device_id=at(dy=dy, dx=dx), device_id_type=MESH)

    loads = []
    for half in range(2):
        first = pl.multiple_of(lax.rem(c + half, 2) * DH, DH)
        loads.append(pltpu.make_async_copy(wg_hbm.at[0, :, pl.ds(first, DH)], WG.at[half], wsem.at[3 * half]))
        loads.append(pltpu.make_async_copy(wu_hbm.at[0, :, pl.ds(first, DH)], WU.at[half], wsem.at[3 * half + 1]))
        loads.append(pltpu.make_async_copy(wd_hbm.at[0, :, pl.ds(first, DH)], WD.at[half], wsem.at[3 * half + 2]))
    for load in loads:
        load.start()

    started = []

    def send(src, dst, device):
        number = len(started)
        copy = pltpu.make_async_remote_copy(
            src_ref=src, dst_ref=dst, send_sem=ssem.at[number], recv_sem=rsem.at[number],
            device_id=device, device_id_type=MESH,
        )
        copy.start()
        started.append(copy)
        return copy

    lane = lax.broadcasted_iota(jnp.int32, (TOK, 128), 1)
    row16 = lax.broadcasted_iota(jnp.int32, (TOK, TOK), 0)
    col16 = lax.broadcasted_iota(jnp.int32, (TOK, TOK), 1)

    def as_column(row):
        spread = jnp.broadcast_to(row.astype(F32), (TOK, TOK))
        return jnp.sum(jnp.where(row16 == col16, spread, 0.0), axis=1, keepdims=True).astype(jnp.int32)

    id_0 = as_column(ids[0:1, :])
    id_1 = as_column(ids[1:2, :])
    marks_0 = jnp.where(lane == id_0, 1.0, 0.0)
    marks_1 = jnp.where(lane == id_1, 1.0, 0.0)
    earlier = jnp.where(col16 < row16, 1.0, 0.0).astype(BF16)
    before = jnp.dot(earlier, (marks_0 + marks_1).astype(BF16), preferred_element_type=F32)
    slot_0 = jnp.sum(before * marks_0, axis=1, keepdims=True)
    slot_1 = jnp.sum(before * marks_1, axis=1, keepdims=True)
    place_0 = (((id_0 - z + NE) & (NE - 1)) * CAP).astype(F32) + slot_0
    place_1 = (((id_1 - z + NE) & (NE - 1)) * CAP).astype(F32) + slot_1
    place = lax.broadcasted_iota(jnp.int32, (TOK, NE * CAP), 1).astype(F32)
    put_0 = jnp.where(place == place_0, 1.0, 0.0)
    put_1 = jnp.where(place == place_1, 1.0, 0.0)
    dispatch = (put_0 + put_1).astype(BF16)
    for q in range(NQ):
        lanes = pl.ds(q * FQ, FQ)
        rows = lax.dot_general(
            dispatch, tokens[:, lanes], (((0,), (0,)), ((), ())), preferred_element_type=F32
        )
        rows = rows.reshape(NE, CAP, FQ).astype(BF16)
        OUT[:, :, lanes] = rows
        ZL[0, :, lanes] = rows[0]
    by_rows = (((1,), (1,)), ((), ()))
    partial = lax.dot_general(tokens[...], router[...], by_rows, preferred_element_type=F32)
    LG[...] = jnp.zeros((TOK, 128), F32)
    LG[:, 0:NE] = partial

    pl.semaphore_wait(barrier, len(column) + len(plane))

    z_moves = []
    for q in range(NQ):
        lanes = pl.ds(q * FQ, FQ)
        z_moves.append(
            [send(OUT.at[j, :, lanes], ZL.at[8 - j, :, lanes], at(dz=j)) for j in (4, 3, 5, 2, 6, 1, 7)]
        )
    logits_move = send(LG, LGR, at(dc=1))

    def small_axis(ab, step):
        return at(dx=step) if ab == 0 else at(dy=step)

    def large_axis(ab, step):
        return at(dy=step) if ab == 0 else at(dx=step)

    near = []
    for q in range(NQ):
        lanes = pl.ds(q * FQ, FQ)
        for move in z_moves[q]:
            move.wait_recv()
        moves = []
        for ab in range(2):
            rows = ZL[4 * ab : 4 * ab + 4, :, lanes].astype(F32).reshape(32, FQ)
            XO[0, ab, 0:32, lanes] = rows.astype(BF16)
            src = XO.at[0, ab, 0:32, lanes]
            moves.append(send(src, XO.at[0, ab, 96:128, lanes], small_axis(ab, 1)))
            moves.append(send(src, XO.at[0, ab, 32:64, lanes], small_axis(ab, 3)))
        near.append(moves)
    far = []
    for q in range(NQ):
        lanes = pl.ds(q * FQ, FQ)
        moves = []
        for ab in range(2):
            near[q][2 * ab].wait_recv()
            moves.append(send(XO.at[0, ab, 96:112, lanes], XO.at[0, ab, 64:80, lanes], small_axis(ab, 1)))
            near[q][2 * ab + 1].wait_recv()
            moves.append(send(XO.at[0, ab, 48:64, lanes], XO.at[0, ab, 80:96, lanes], small_axis(ab, 3)))
        far.append(moves)
    near = []
    across = {}
    for q in range(NQ):
        lanes = pl.ds(q * FQ, FQ)
        moves = []
        for ab in range(2):
            far[q][2 * ab].wait_recv()
            far[q][2 * ab + 1].wait_recv()
            moves.append(send(XO.at[0, ab, :, lanes], XO.at[3, ab, :, lanes], large_axis(ab, 1)))
            moves.append(send(XO.at[0, ab, :, lanes], XO.at[1, ab, :, lanes], large_axis(ab, 3)))
        near.append(moves)
        across[0, q] = send(XO.at[0, :, :, lanes], XP.at[0, :, :, lanes], at(dc=1))

    for load in loads:
        load.wait()

    partner_sums = {}

    def compute(rel):
        own = XO[rel].reshape(256, DH)
        other = XP[rel].reshape(256, DH)
        gate = lax.dot_general(WG[0], own, by_rows, preferred_element_type=F32)
        gate += lax.dot_general(WG[1], other, by_rows, preferred_element_type=F32)
        up = lax.dot_general(WU[0], own, by_rows, preferred_element_type=F32)
        up += lax.dot_general(WU[1], other, by_rows, preferred_element_type=F32)
        H[...] = (gate * jax.nn.sigmoid(gate) * up).T.astype(BF16)

        def down_other(n, carry):
            cols = pl.ds(pl.multiple_of(n * 256, 256), 256)
            PX[rel, :, cols] = jnp.dot(H[...], WD[1, :, cols], preferred_element_type=F32).astype(BF16)
            return carry

        def down_own(n, carry):
            cols = pl.ds(pl.multiple_of(n * 256, 256), 256)
            PO[rel, :, cols] = jnp.dot(H[...], WD[0, :, cols], preferred_element_type=F32)
            return carry

        lax.fori_loop(0, DH // 256, down_other, 0)
        partner_sums[rel] = send(PX.at[rel], PR.at[rel], at(dc=1))
        lax.fori_loop(0, DH // 256, down_own, 0)

    for q in range(NQ):
        across[0, q].wait_recv()
    compute(0)

    far = []
    for q in range(NQ):
        lanes = pl.ds(q * FQ, FQ)
        moves = []
        for ab in range(2):
            near[q][2 * ab].wait_recv()
            moves.append(send(XO.at[3, ab, 0:64, lanes], XO.at[2, ab, 0:64, lanes], large_axis(ab, 1)))
            near[q][2 * ab + 1].wait_recv()
            moves.append(send(XO.at[1, ab, 64:128, lanes], XO.at[2, ab, 64:128, lanes], large_axis(ab, 3)))
        far.append(moves)
        for rel in (1, 3):
            across[rel, q] = send(XO.at[rel, :, :, lanes], XP.at[rel, :, :, lanes], at(dc=1))
    for rel in (1, 3):
        for q in range(NQ):
            across[rel, q].wait_recv()
        compute(rel)
    for q in range(NQ):
        lanes = pl.ds(q * FQ, FQ)
        for move in far[q]:
            move.wait_recv()
        across[2, q] = send(XO.at[2, :, :, lanes], XP.at[2, :, :, lanes], at(dc=1))

    direct = {}
    for rel in (1, 3):
        partner_sums[rel].wait_recv()
        S[rel] = (PO[rel] + PR[rel].astype(F32)).astype(BF16).reshape(2, 128, DH)
        for q in range(NQ):
            lanes = pl.ds(q * FQ, FQ)
            for ab in range(2):
                half = slice(64, 128) if rel == 1 else slice(0, 64)
                slot = 0 if rel == 1 else 1
                direct[rel, q, ab] = send(
                    S.at[rel, ab, half, lanes], R2.at[slot, ab, half, lanes], large_axis(ab, rel)
                )
    for q in range(NQ):
        across[2, q].wait_recv()
    compute(2)
    partner_sums[0].wait_recv()
    partner_sums[2].wait_recv()
    first = {}
    for q in range(NQ):
        lanes = pl.ds(q * FQ, FQ)
        S[2, :, :, lanes] = (PO[2, :, lanes] + PR[2, :, lanes].astype(F32)).astype(BF16).reshape(2, 128, FQ)
        for ab in range(2):
            first[q, ab, 1] = send(S.at[2, ab, 0:64, lanes], R1.at[ab, 0:64, lanes], large_axis(ab, 1))
            first[q, ab, 3] = send(S.at[2, ab, 64:128, lanes], R1.at[ab, 64:128, lanes], large_axis(ab, 3))
    second = {}
    for q in range(NQ):
        lanes = pl.ds(q * FQ, FQ)
        for ab in range(2):
            for rel, half, slot in ((1, slice(0, 64), 0), (3, slice(64, 128), 1)):
                first[q, ab, rel].wait_recv()
                S[rel, ab, half, lanes] = (
                    S[rel, ab, half, lanes].astype(F32) + R1[ab, half, lanes].astype(F32)
                ).astype(BF16)
                second[q, ab, rel] = send(
                    S.at[rel, ab, half, lanes], R2.at[slot, ab, half, lanes], large_axis(ab, rel)
                )
    direct_small = {}
    first_small = {}
    for q in range(NQ):
        lanes = pl.ds(q * FQ, FQ)
        for ab in range(2):
            block = slice(128 * ab, 128 * ab + 128)
            for rel in (1, 3):
                direct[rel, q, ab].wait_recv()
                second[q, ab, rel].wait_recv()
            total = PO[0, block, lanes] + PR[0, block, lanes].astype(F32)
            total += R2[0, ab, :, lanes].astype(F32)
            total += R2[1, ab, :, lanes].astype(F32)
            PO[0, block, lanes] = total
            TB[ab, :, lanes] = total.astype(BF16)
            first_small[q, ab, 1] = send(TB.at[ab, 64:80, lanes], T1.at[ab, 0:16, lanes], small_axis(ab, 1))
            first_small[q, ab, 3] = send(TB.at[ab, 80:96, lanes], T1.at[ab, 16:32, lanes], small_axis(ab, 3))
            direct_small[q, ab, 1] = send(TB.at[ab, 48:64, lanes], T2.at[0, ab, 16:32, lanes], small_axis(ab, 1))
            direct_small[q, ab, 3] = send(TB.at[ab, 96:112, lanes], T2.at[1, ab, 0:16, lanes], small_axis(ab, 3))
    second_small = {}
    for q in range(NQ):
        lanes = pl.ds(q * FQ, FQ)
        for ab in range(2):
            for rel, base, half, slot in ((1, 32, slice(0, 16), 0), (3, 96, slice(16, 32), 1)):
                first_small[q, ab, rel].wait_recv()
                mine = slice(base + half.start, base + half.stop)
                TB[ab, mine, lanes] = (
                    PO[0, 128 * ab + mine.start : 128 * ab + mine.stop, lanes] + T1[ab, half, lanes].astype(F32)
                ).astype(BF16)
                second_small[q, ab, rel] = send(
                    TB.at[ab, mine, lanes], T2.at[slot, ab, half, lanes], small_axis(ab, rel)
                )
    returns = []
    for q in range(NQ):
        lanes = pl.ds(q * FQ, FQ)
        for ab in range(2):
            for rel in (1, 3):
                direct_small[q, ab, rel].wait_recv()
                second_small[q, ab, rel].wait_recv()
            total = PO[0, 128 * ab : 128 * ab + 32, lanes]
            total += T2[0, ab, :, lanes].astype(F32)
            total += T2[1, ab, :, lanes].astype(F32)
            RET[4 * ab : 4 * ab + 4, :, lanes] = total.reshape(4, CAP, FQ).astype(BF16)
        BACK[0, :, lanes] = RET[0, :, lanes]
        returns.append(
            [send(RET.at[j, :, lanes], BACK.at[8 - j, :, lanes], at(dz=j)) for j in (4, 3, 5, 2, 6, 1, 7)]
        )

    logits_move.wait_recv()
    logits = LG[...] + LGR[...]
    picked_0 = jnp.sum(logits * marks_0, axis=1, keepdims=True)
    picked_1 = jnp.sum(logits * marks_1, axis=1, keepdims=True)
    gate_0 = jax.nn.sigmoid(picked_0 - picked_1)
    gate_1 = jax.nn.sigmoid(picked_1 - picked_0)
    weights = gate_0 * put_0 + gate_1 * put_1
    high = weights.astype(BF16)
    rest = weights - high.astype(F32)
    middle = rest.astype(BF16)
    low = (rest - middle.astype(F32)).astype(BF16)
    parts = jnp.concatenate([high, middle, low], axis=0)

    counted = lengths[...].astype(F32)
    row64 = lax.broadcasted_iota(jnp.int32, (NSEQ, NSEQ), 0)
    col64 = lax.broadcasted_iota(jnp.int32, (NSEQ, NSEQ), 1)
    upto = jnp.where(row64 <= col64, 1.0, 0.0).astype(BF16)
    wide = jnp.broadcast_to(counted, (8, NSEQ)).astype(BF16)
    ends = jnp.dot(wide, upto, preferred_element_type=F32)[0:1]
    starts = ends - counted
    first_token = ((y * 4 + x) * 8 + z) * TOK
    position = (first_token + lax.broadcasted_iota(jnp.int32, (TOK, NSEQ), 0)).astype(F32)
    inside = jnp.where((position >= starts) & (position < ends), 1.0, 0.0).astype(BF16)
    closing = jnp.max(jnp.where(position + 1.0 == ends, 1.0, 0.0), axis=1, keepdims=True)
    bench_row = lax.broadcasted_iota(jnp.int32, (128, NSEQ), 0)
    table = jnp.where(bench_row == bench[...], 1.0, 0.0).astype(BF16)
    bench_of = lax.dot_general(inside, table, by_rows, preferred_element_type=F32)
    bench_of = bench_of * (1.0 - closing)
    less_one = jnp.broadcast_to(counted - 1.0, (8, NSEQ)).astype(BF16)
    counts = lax.dot_general(less_one, table, by_rows, preferred_element_type=F32)[0:1]

    token_sum = jnp.zeros((TOK, 1), F32)
    for q in range(NQ):
        lanes = pl.ds(q * FQ, FQ)
        for move in returns[q]:
            move.wait_recv()
        back = BACK[:, :, lanes].astype(F32).reshape(NE * CAP, FQ).astype(BF16)
        three = jnp.dot(parts, back, preferred_element_type=F32)
        mixed = (three[0:16] + (three[16:32] + three[32:48])).astype(BF16)
        mixed_out[:, lanes] = mixed
        diff = mixed.astype(F32) - target[:, lanes].astype(F32)
        token_sum += jnp.sum(diff * diff, axis=1, keepdims=True)
    sums = jnp.sum(bench_of * (token_sum / D), axis=0, keepdims=True)

    mine = z * 2 + c
    L1[mine] = jnp.broadcast_to(sums, (8, 128))
    moves = [send(L1.at[mine], L1.at[mine], at(dz=dz, dc=dc)) for dz, dc in column]
    for move in moves:
        move.wait_recv()
    mine = y * 4 + x
    L2[mine] = jnp.sum(L1[...], axis=0)
    moves = [send(L2.at[mine], L2.at[mine], at(dy=dy, dx=dx)) for dy, dx in plane]
    for move in moves:
        move.wait_recv()
    loss_sum = jnp.sum(L2[...], axis=0)[0:1]
    loss_out[...] = (loss_sum / jnp.maximum(counts, 1.0))[:, 0:NB]
    counts_out[...] = counts[:, 0:NB].astype(jnp.int32)
    for copy in started:
        copy.wait_send()


def per_device(tokens, target, router, w_gate, w_up, w_down, expert_ids, lengths, bench_ids):
    vmem = pl.BlockSpec(memory_space=pltpu.VMEM)
    hbm = pl.BlockSpec(memory_space=pl.ANY)
    mixed, loss, counts = pl.pallas_call(
        kernel,
        name="moe",
        out_shape=(
            jax.ShapeDtypeStruct((TOK, DH), BF16),
            jax.ShapeDtypeStruct((1, NB), F32),
            jax.ShapeDtypeStruct((1, NB), jnp.int32),
        ),
        in_specs=[vmem, vmem, vmem, hbm, hbm, hbm, vmem, vmem, vmem],
        out_specs=(vmem, vmem, vmem),
        scratch_shapes=[
            pltpu.VMEM((NE, CAP, DH), BF16),
            pltpu.VMEM((NE, CAP, DH), BF16),
            pltpu.VMEM((4, 2, 128, DH), BF16),
            pltpu.VMEM((4, 2, 128, DH), BF16),
            pltpu.VMEM((2, HID, DH), BF16),
            pltpu.VMEM((2, HID, DH), BF16),
            pltpu.VMEM((2, HID, DH), BF16),
            pltpu.VMEM((256, HID), BF16),
            pltpu.VMEM((4, 256, DH), BF16),
            pltpu.VMEM((4, 256, DH), BF16),
            pltpu.VMEM((4, 256, DH), F32),
            pltpu.VMEM((4, 2, 128, DH), BF16),
            pltpu.VMEM((2, 128, DH), BF16),
            pltpu.VMEM((2, 2, 128, DH), BF16),
            pltpu.VMEM((2, 128, DH), BF16),
            pltpu.VMEM((2, 32, DH), BF16),
            pltpu.VMEM((2, 2, 32, DH), BF16),
            pltpu.VMEM((NE, CAP, DH), BF16),
            pltpu.VMEM((NE, CAP, DH), BF16),
            pltpu.VMEM((TOK, 128), F32),
            pltpu.VMEM((TOK, 128), F32),
            pltpu.VMEM((16, 8, 128), F32),
            pltpu.VMEM((16, 8, 128), F32),
            pltpu.VMEM((8, 128), F32),
            pltpu.SemaphoreType.DMA((6,)),
            pltpu.SemaphoreType.DMA((NSEMS,)),
            pltpu.SemaphoreType.DMA((NSEMS,)),
        ],
        compiler_params=pltpu.CompilerParams(
            collective_id=0, has_side_effects=True, vmem_limit_bytes=66 * 1000 * 1000
        ),
    )(
        tokens, target, router.T, w_gate.swapaxes(1, 2), w_up.swapaxes(1, 2), w_down, expert_ids.T,
        lengths.reshape(1, NSEQ), bench_ids.reshape(1, NSEQ),
    )
    return (mixed, loss.reshape(NB), counts.reshape(NB))


def solution(mesh):
    split = Mesh(
        mesh.devices.reshape(4, 4, mesh.shape["expert"], mesh.shape["tensor"]),
        ("dp_0", "dp_1", "expert", "tensor"),
    )
    in_specs = (
        P(DP_EXPERT, "tensor"),
        P(DP_EXPERT, "tensor"),
        P("tensor", None),
        P("expert", None, DP_TENSOR),
        P("expert", None, DP_TENSOR),
        P("expert", DP_TENSOR, None),
        P(DP_EXPERT, None),
        P(),
        P(),
    )
    out_specs = (P(DP_EXPERT, "tensor"), P(), P())
    return jax.shard_map(
        per_device, mesh=split, in_specs=in_specs, out_specs=out_specs, check_vma=False
    )
```

time: 318 us -> 104 us (0.33)
  waiting for transfers between devices: 194 us -> 0 us
  Pallas kernels: 0 us -> 99.8 us
  blocking collectives: 68.7 us -> 0 us
  matrix products: 25.9 us -> 0 us
  between operations: 14.2 us -> 0.64 us
  starting transfers between devices: 6.86 us -> 0 us
    reduce_scatter x1 -> x0, waiting for transfers between devices: 111 us -> none  [per_device(): lax.psum_scatter(jnp.dot(hidden, down_w, preferred_element_type=jnp.float...]
    pallas_call x0 -> x1, Pallas kernels: none -> 99.8 us  [per_device(): pl.pallas_call(kernel, name='moe', out_shape=(jax.ShapeDtypeStruct((TOK,...]
    all_gather x1 -> x0, waiting for transfers between devices: 71.8 us -> none  [per_device(): every_row = lax.all_gather(whole, DP, axis=0, tiled=True).reshape(-1, D)]
    psum x5 -> x0, blocking collectives: 40.1 us -> none  [the longest x4 37.2 us: one_axis_at_a_time(): shard = lax.psum(shard, axis)]
    dot_general x8 -> x0, matrix products: 25.9 us -> none  [the longest x1 16.5 us: per_device(): jnp.dot(hidden, down_w, preferred_element_type=jnp.float32)]
    all_to_all x2 -> x0, blocking collectives: 24.4 us -> none  [the longest x1 19.3 us: per_device(): lax.all_to_all(outgoing, 'expert', split_axis=1, concat_axis=1, tiled=True)]
    all_to_all x1 -> x0, waiting for transfers between devices: 10.7 us -> none  [per_device(): lax.all_to_all(results, 'expert', split_axis=1, concat_axis=1, tiled=True)]
    all_to_all x1 -> x0, starting transfers between devices: 6.78 us -> none  [per_device(): lax.all_to_all(results, 'expert', split_axis=1, concat_axis=1, tiled=True)]
  transfers between devices with their start and end apart: 3 -> 0, of which waited for: 3 -> 0; matrix products, arithmetic and copies ran while one was open for 0% -> 0% of each run, Pallas kernels for 0% -> 0%
where the time goes in v1:
time: 104 us
  Pallas kernels  99.8 us (96%)
  local copies, waits for them, and re-layouts  3.7 us (4%)
    pallas_call x1, Pallas kernels, per_device(): pl.pallas_call(kernel, name='moe', out_shape=(jax.ShapeDtypeStruct((TOK,...  99.8 us
    unnamed x3, local copies, waits for them, and re-layouts  3.7 us

profile of v1, /device:TPU:1, one launch (start us, length us, event | category | flops | bytes accessed | tf_op | source)
XLA Modules:
  0.0 104.1 jit_solution(15188757966361499860)
XLA Ops:
  0.6 99.8 %moe.1 = (bf16[16,2048]{1,0:T(8,128)(2,1)}, f32[1,16]{1,0:T(1,128)}, s32[1,16]{1,0:T(1,128)}) custom-call(bf16[16,2048]{1,0:T(8,128)(2,1)} %tokens.1, bf16[16,2048]{1,0:T(8,128)(2,1)} %target.1, bf16[8,2048]{1,0:T(8,128)(2,1)} %bitcast.10, bf16[1,448,4096]{2,1,0:T(8,128)(2,1)} %bitcast.8, bf16[1,448,4096]{2,1,0:T(8,128)(2,1)} %bitcast.9, ...), custom_call_target="tpu_custom_call" | custom-call | tf_op jit(solution)/shard_map/moe/pallas_call | solution.py:363
  100.4 1.5 %copy.15 = bf16[16,2048]{1,0:T(8,128)(2,1)} copy(bf16[16,2048]{1,0:T(8,128)(2,1)} %get-tuple-element.12) | data formatting | bytes 131072
  101.9 1.1 %copy.16 = f32[16]{0:T(128)} copy(f32[16]{0:T(128)} %bitcast.15) | data formatting | bytes 128
  103.0 1.1 %copy.17 = s32[16]{0:T(128)} copy(s32[16]{0:T(128)} %bitcast.14) | data formatting | bytes 128

commit v2 on v1

v2 whole, which is shorter than its diff:
```python
import jax
import jax.numpy as jnp
from jax import lax
from jax.experimental import pallas as pl
from jax.experimental.pallas import tpu as pltpu
from jax.sharding import Mesh
from jax.sharding import PartitionSpec as P

D = 4096
DH = D // 2
NB = 16
CAP = 8
TOK = 16
HID = 448
NSEQ = 64
NE = 8
NQ = 2
FQ = DH // NQ
DP_EXPERT = ("dp_0", "dp_1", "expert")
DP_TENSOR = ("dp_0", "dp_1", "tensor")
MESH = pl.DeviceIdType.MESH
F32 = jnp.float32
BF16 = jnp.bfloat16
NSEMS = 19 * NQ + 3


def kernel(
    tokens_hbm, target_hbm, router_hbm, wg_hbm, wu_hbm, wd_hbm, ids_hbm, lengths_hbm, bench_hbm,
    mixed_hbm, loss_out, counts_out,
    tokens, target, router, ids, lengths, bench, mixed_out,
    OUT, ZL, XO, XP, WG, WU, WD, H, PX, PR, PO, S, R1, R2, TB, T1, T2, RET, BACK,
    LG, LGR, L1, L2, wsem, ssem, rsem,
):
    y = lax.axis_index("dp_0")
    x = lax.axis_index("dp_1")
    z = lax.axis_index("expert")
    c = lax.axis_index("tensor")

    def at(dy=0, dx=0, dz=0, dc=0):
        return {
            "dp_0": lax.rem(y + dy, 4),
            "dp_1": lax.rem(x + dx, 4),
            "expert": lax.rem(z + dz, 8),
            "tensor": lax.rem(c + dc, 2),
        }

    column = [(dz, dc) for dz in range(8) for dc in range(2)][1:]
    plane = [(dy, dx) for dy in range(4) for dx in range(4)][1:]
    barrier = pltpu.get_barrier_semaphore()
    for dz, dc in column:
        pl.semaphore_signal(barrier, inc=1, device_id=at(dz=dz, dc=dc), device_id_type=MESH)
    for dy, dx in plane:
        pl.semaphore_signal(barrier, inc=1, device_id=at(dy=dy, dx=dx), device_id_type=MESH)

    inputs = (
        (ids_hbm, ids), (tokens_hbm, tokens), (router_hbm, router),
        (target_hbm, target), (lengths_hbm, lengths), (bench_hbm, bench),
    )
    inputs = [pltpu.make_async_copy(src, dst, wsem.at[6 + i]) for i, (src, dst) in enumerate(inputs)]
    for copy in inputs:
        copy.start()
    loads = []
    for half in range(2):
        first = pl.multiple_of(lax.rem(c + half, 2) * DH, DH)
        loads.append(pltpu.make_async_copy(wg_hbm.at[0, :, pl.ds(first, DH)], WG.at[half], wsem.at[3 * half]))
        loads.append(pltpu.make_async_copy(wu_hbm.at[0, :, pl.ds(first, DH)], WU.at[half], wsem.at[3 * half + 1]))
        loads.append(pltpu.make_async_copy(wd_hbm.at[0, :, pl.ds(first, DH)], WD.at[half], wsem.at[3 * half + 2]))
    for load in loads:
        load.start()

    waits, numbers = [], {}

    def send(group, src, dst, device):
        number = numbers.setdefault(group, len(numbers))
        pltpu.make_async_remote_copy(
            src_ref=src, dst_ref=dst, send_sem=ssem.at[number], recv_sem=rsem.at[number],
            device_id=device, device_id_type=MESH,
        ).start()

    def arrived(group, region):
        number = numbers[group]
        copies = pltpu.make_async_remote_copy(
            src_ref=region, dst_ref=region, send_sem=ssem.at[number], recv_sem=rsem.at[number],
            device_id=at(dc=1), device_id_type=MESH,
        )
        copies.wait_recv()
        waits.append(copies)

    for copy in inputs:
        copy.wait()
    lane = lax.broadcasted_iota(jnp.int32, (TOK, 128), 1)
    row16 = lax.broadcasted_iota(jnp.int32, (TOK, TOK), 0)
    col16 = lax.broadcasted_iota(jnp.int32, (TOK, TOK), 1)

    def as_column(row):
        spread = jnp.broadcast_to(row.astype(F32), (TOK, TOK))
        return jnp.sum(jnp.where(row16 == col16, spread, 0.0), axis=1, keepdims=True).astype(jnp.int32)

    id_0 = as_column(ids[0:1, :])
    id_1 = as_column(ids[1:2, :])
    marks_0 = jnp.where(lane == id_0, 1.0, 0.0)
    marks_1 = jnp.where(lane == id_1, 1.0, 0.0)
    earlier = jnp.where(col16 < row16, 1.0, 0.0).astype(BF16)
    before = jnp.dot(earlier, (marks_0 + marks_1).astype(BF16), preferred_element_type=F32)
    slot_0 = jnp.sum(before * marks_0, axis=1, keepdims=True)
    slot_1 = jnp.sum(before * marks_1, axis=1, keepdims=True)
    place_0 = (((id_0 - z + NE) & (NE - 1)) * CAP).astype(F32) + slot_0
    place_1 = (((id_1 - z + NE) & (NE - 1)) * CAP).astype(F32) + slot_1
    place = lax.broadcasted_iota(jnp.int32, (TOK, NE * CAP), 1).astype(F32)
    put_0 = jnp.where(place == place_0, 1.0, 0.0)
    put_1 = jnp.where(place == place_1, 1.0, 0.0)
    dispatch = (put_0 + put_1).astype(BF16)
    for q in range(NQ):
        lanes = pl.ds(q * FQ, FQ)
        rows = lax.dot_general(
            dispatch, tokens[:, lanes], (((0,), (0,)), ((), ())), preferred_element_type=F32
        )
        rows = rows.reshape(NE, CAP, FQ).astype(BF16)
        OUT[:, :, lanes] = rows
        ZL[0, :, lanes] = rows[0]
    by_rows = (((1,), (1,)), ((), ()))
    partial = lax.dot_general(tokens[...], router[...], by_rows, preferred_element_type=F32)
    LG[...] = jnp.zeros((TOK, 128), F32)
    LG[:, 0:NE] = partial

    pl.semaphore_wait(barrier, len(column) + len(plane))

    for q in range(NQ):
        lanes = pl.ds(q * FQ, FQ)
        for j in (4, 3, 5, 2, 6, 1, 7):
            send(("z", q), OUT.at[j, :, lanes], ZL.at[8 - j, :, lanes], at(dz=j))
    send("logits", LG, LGR, at(dc=1))

    def small_axis(ab, step):
        return at(dx=step) if ab == 0 else at(dy=step)

    def large_axis(ab, step):
        return at(dy=step) if ab == 0 else at(dx=step)

    def wavefront(stages, lags):
        for tick in range(NQ + lags[-1]):
            for stage, lag in zip(stages, lags):
                if 0 <= tick - lag < NQ:
                    stage(tick - lag, pl.ds((tick - lag) * FQ, FQ))

    def from_z(q, lanes):
        arrived(("z", q), ZL.at[1:8, :, lanes])
        for ab in range(2):
            rows = ZL[4 * ab : 4 * ab + 4, :, lanes].astype(F32).reshape(32, FQ)
            XO[0, ab, 0:32, lanes] = rows.astype(BF16)
            src = XO.at[0, ab, 0:32, lanes]
            send(("near_small", q), src, XO.at[0, ab, 96:128, lanes], small_axis(ab, 1))
            send(("near_small", q), src, XO.at[0, ab, 32:64, lanes], small_axis(ab, 3))

    def small_forward(q, lanes):
        arrived(("near_small", q), XO.at[0, :, 0:64, lanes])
        for ab in range(2):
            send(
                ("far_small", q), XO.at[0, ab, 96:112, lanes], XO.at[0, ab, 64:80, lanes], small_axis(ab, 1)
            )
            send(
                ("far_small", q), XO.at[0, ab, 48:64, lanes], XO.at[0, ab, 80:96, lanes], small_axis(ab, 3)
            )

    def to_partner(unit, q, lanes):
        send(("across", unit, q), XO.at[unit, :, :, lanes], XP.at[unit, :, :, lanes], at(dc=1))

    def large_own(q, lanes):
        arrived(("far_small", q), XO.at[0, :, 0:32, lanes])
        for ab in range(2):
            upper, lower = XO.at[0, ab, 0:64, lanes], XO.at[0, ab, 64:128, lanes]
            send(("near", q), upper, XO.at[1, ab, 0:64, lanes], large_axis(ab, 1))
            send(("near", q), lower, XO.at[1, ab, 64:128, lanes], large_axis(ab, 3))
        to_partner(0, q, lanes)

    def large_forward(q, lanes):
        arrived(("near", q), XO.at[1, :, :, lanes])
        for ab in range(2):
            send(("far", q), XO.at[1, ab, 0:64, lanes], XO.at[2, ab, 0:64, lanes], large_axis(ab, 1))
            send(("far", q), XO.at[1, ab, 64:128, lanes], XO.at[2, ab, 64:128, lanes], large_axis(ab, 3))
        to_partner(1, q, lanes)

    wavefront((from_z, small_forward, large_own), (0, 1, 2))
    halves = [(q, pl.ds(q * FQ, FQ)) for q in range(NQ)]
    large_forward(*halves[0])

    for load in loads:
        load.wait()

    def up(unit):
        for q, lanes in halves:
            arrived(("across", unit, q), XP.at[unit, :, :, lanes])
        own = XO[unit].reshape(256, DH)
        other = XP[unit].reshape(256, DH)
        gate = lax.dot_general(WG[0], own, by_rows, preferred_element_type=F32)
        gate += lax.dot_general(WG[1], other, by_rows, preferred_element_type=F32)
        raise_ = lax.dot_general(WU[0], own, by_rows, preferred_element_type=F32)
        raise_ += lax.dot_general(WU[1], other, by_rows, preferred_element_type=F32)
        H[...] = (gate * jax.nn.sigmoid(gate) * raise_).astype(BF16).T

    def down(unit):
        for q, lanes in halves:
            for n in range(q * FQ, q * FQ + FQ, 512):
                cols = slice(n, n + 512)
                PX[unit, :, cols] = jnp.dot(H[...], WD[1, :, cols], preferred_element_type=F32).astype(BF16)
            send(("sums", unit, q), PX.at[unit, :, lanes], PR.at[unit, :, lanes], at(dc=1))
        for n in range(0, DH, 512):
            cols = slice(n, n + 512)
            PO[unit, :, cols] = jnp.dot(H[...], WD[0, :, cols], preferred_element_type=F32)

    def chip_sum(unit, q, lanes):
        arrived(("sums", unit, q), PR.at[unit, :, lanes])
        return PO[unit, :, lanes] + PR[unit, :, lanes].astype(F32)

    up(0)
    large_forward(*halves[1])
    for q, lanes in halves:
        for ab in range(2):
            upper, lower = XO.at[0, ab, 0:64, lanes], XO.at[0, ab, 64:128, lanes]
            send(("late", q), lower, XO.at[3, ab, 64:128, lanes], large_axis(ab, 1))
            send(("late", q), upper, XO.at[3, ab, 0:64, lanes], large_axis(ab, 3))
    down(0)
    up(1)
    down(1)
    for q, lanes in halves:
        arrived(("far", q), XO.at[2, :, :, lanes])
        to_partner(2, q, lanes)
    for q, lanes in halves:
        S[0, :, :, lanes] = chip_sum(1, q, lanes).astype(BF16).reshape(2, 128, FQ)
        for ab in range(2):
            send(("sent", q), S.at[0, ab, 64:128, lanes], R2.at[0, ab, 64:128, lanes], large_axis(ab, 1))
            send(("sent", q), S.at[0, ab, 0:64, lanes], R2.at[1, ab, 0:64, lanes], large_axis(ab, 3))
    up(2)
    for q, lanes in halves:
        arrived(("late", q), XO.at[3, :, :, lanes])
        to_partner(3, q, lanes)
    down(2)
    for q, lanes in halves:
        S[1, :, :, lanes] = chip_sum(2, q, lanes).astype(BF16).reshape(2, 128, FQ)
        for ab in range(2):
            send(("first", q), S.at[1, ab, 0:64, lanes], R1.at[ab, 0:64, lanes], large_axis(ab, 1))
            send(("first", q), S.at[1, ab, 64:128, lanes], R1.at[ab, 64:128, lanes], large_axis(ab, 3))
    up(3)
    down(3)
    arrived("logits", LGR)
    logits = LG[...] + LGR[...]
    picked_0 = jnp.sum(logits * marks_0, axis=1, keepdims=True)
    picked_1 = jnp.sum(logits * marks_1, axis=1, keepdims=True)
    gate_0 = jax.nn.sigmoid(picked_0 - picked_1)
    gate_1 = jax.nn.sigmoid(picked_1 - picked_0)
    weights = gate_0 * put_0 + gate_1 * put_1
    high = weights.astype(BF16)
    rest = weights - high.astype(F32)
    middle = rest.astype(BF16)
    low = (rest - middle.astype(F32)).astype(BF16)
    parts = jnp.concatenate([high, middle, low], axis=0)

    counted = lengths[...].astype(F32)
    row64 = lax.broadcasted_iota(jnp.int32, (NSEQ, NSEQ), 0)
    col64 = lax.broadcasted_iota(jnp.int32, (NSEQ, NSEQ), 1)
    upto = jnp.where(row64 <= col64, 1.0, 0.0).astype(BF16)
    wide = jnp.broadcast_to(counted, (8, NSEQ)).astype(BF16)
    ends = jnp.dot(wide, upto, preferred_element_type=F32)[0:1]
    starts = ends - counted
    first_token = ((y * 4 + x) * 8 + z) * TOK
    position = (first_token + lax.broadcasted_iota(jnp.int32, (TOK, NSEQ), 0)).astype(F32)
    inside = jnp.where((position >= starts) & (position < ends), 1.0, 0.0).astype(BF16)
    closing = jnp.max(jnp.where(position + 1.0 == ends, 1.0, 0.0), axis=1, keepdims=True)
    bench_row = lax.broadcasted_iota(jnp.int32, (128, NSEQ), 0)
    table = jnp.where(bench_row == bench[...], 1.0, 0.0).astype(BF16)
    bench_of = lax.dot_general(inside, table, by_rows, preferred_element_type=F32)
    bench_of = bench_of * (1.0 - closing)
    less_one = jnp.broadcast_to(counted - 1.0, (8, NSEQ)).astype(BF16)
    counts = lax.dot_general(less_one, table, by_rows, preferred_element_type=F32)[0:1]

    for q, lanes in halves:
        total = chip_sum(3, q, lanes)
        arrived(("first", q), R1.at[:, :, lanes])
        S[2, :, :, lanes] = (total.reshape(2, 128, FQ) + R1[:, :, lanes].astype(F32)).astype(BF16)
        for ab in range(2):
            send(("sent", q), S.at[2, ab, 0:64, lanes], R2.at[0, ab, 0:64, lanes], large_axis(ab, 1))
            send(("sent", q), S.at[2, ab, 64:128, lanes], R2.at[1, ab, 64:128, lanes], large_axis(ab, 3))
    for q, lanes in halves:
        PO[0, :, lanes] = chip_sum(0, q, lanes)
    token_sums = []

    def large_total(q, lanes):
        arrived(("sent", q), R2.at[:, :, :, lanes])
        for ab in range(2):
            block = slice(128 * ab, 128 * ab + 128)
            total = PO[0, block, lanes] + R2[0, ab, :, lanes].astype(F32)
            total += R2[1, ab, :, lanes].astype(F32)
            PO[0, block, lanes] = total
            TB[ab, :, lanes] = total.astype(BF16)
            send(("first_small", q), TB.at[ab, 64:80, lanes], T1.at[ab, 0:16, lanes], small_axis(ab, 1))
            send(("first_small", q), TB.at[ab, 80:96, lanes], T1.at[ab, 16:32, lanes], small_axis(ab, 3))
            send(("sent_small", q), TB.at[ab, 48:64, lanes], T2.at[0, ab, 16:32, lanes], small_axis(ab, 1))
            send(("sent_small", q), TB.at[ab, 96:112, lanes], T2.at[1, ab, 0:16, lanes], small_axis(ab, 3))

    def small_step(q, lanes):
        arrived(("first_small", q), T1.at[:, :, lanes])
        for ab in range(2):
            for rel, base, half, slot in ((1, 32, slice(0, 16), 0), (3, 96, slice(16, 32), 1)):
                rows = slice(base + half.start, base + half.stop)
                TB[ab, rows, lanes] = (
                    PO[0, 128 * ab + rows.start : 128 * ab + rows.stop, lanes] + T1[ab, half, lanes].astype(F32)
                ).astype(BF16)
                send(
                    ("sent_small", q), TB.at[ab, rows, lanes], T2.at[slot, ab, half, lanes], small_axis(ab, rel)
                )

    def small_total(q, lanes):
        arrived(("sent_small", q), T2.at[:, :, :, lanes])
        for ab in range(2):
            total = PO[0, 128 * ab : 128 * ab + 32, lanes]
            total += T2[0, ab, :, lanes].astype(F32)
            total += T2[1, ab, :, lanes].astype(F32)
            RET[4 * ab : 4 * ab + 4, :, lanes] = total.reshape(4, CAP, FQ).astype(BF16)
        BACK[0, :, lanes] = RET[0, :, lanes]
        for j in (4, 3, 5, 2, 6, 1, 7):
            send(("back", q), RET.at[j, :, lanes], BACK.at[8 - j, :, lanes], at(dz=j))

    def mix(q, lanes):
        arrived(("back", q), BACK.at[1:8, :, lanes])
        back = BACK[:, :, lanes].astype(F32).reshape(NE * CAP, FQ).astype(BF16)
        three = jnp.dot(parts, back, preferred_element_type=F32)
        mixed = (three[0:16] + (three[16:32] + three[32:48])).astype(BF16)
        mixed_out[:, lanes] = mixed
        diff = mixed.astype(F32) - target[:, lanes].astype(F32)
        token_sums.append(jnp.sum(diff * diff, axis=1, keepdims=True))

    wavefront((large_total, small_step, small_total, mix), (0, 1, 2, 4))
    token_sum = sum(token_sums[1:], token_sums[0])
    sums = jnp.sum(bench_of * (token_sum / D), axis=0, keepdims=True)

    hand = pltpu.make_async_copy(mixed_out, mixed_hbm, wsem.at[12])
    hand.start()
    mine = z * 2 + c
    L1[mine] = sums
    for dz, dc in column:
        send("column", L1.at[mine], L1.at[mine], at(dz=dz, dc=dc))
    arrived("column", L1.at[0:15])
    mine = y * 4 + x
    L2[mine] = jnp.sum(L1[...], axis=0)
    for dy, dx in plane:
        send("plane", L2.at[mine], L2.at[mine], at(dy=dy, dx=dx))
    arrived("plane", L2.at[0:15])
    loss_sum = jnp.sum(L2[...], axis=0)
    loss_out[...] = (loss_sum / jnp.maximum(counts, 1.0))[:, 0:NB]
    counts_out[...] = counts[:, 0:NB].astype(jnp.int32)
    hand.wait()
    for copy in waits:
        copy.wait_send()


def hand_over(*refs):
    sources, targets, stages, sems = refs[0:3], refs[3:6], refs[6:9], refs[9]
    arriving = [pltpu.make_async_copy(sources[i], stages[i], sems.at[i]) for i in range(3)]
    leaving = [pltpu.make_async_copy(stages[i], targets[i], sems.at[3 + i]) for i in range(3)]
    for copy in arriving:
        copy.start()
    for i in range(3):
        arriving[i].wait()
        leaving[i].start()
    for copy in leaving:
        copy.wait()


def per_device(tokens, target, router, w_gate, w_up, w_down, expert_ids, lengths, bench_ids):
    vmem = pl.BlockSpec(memory_space=pltpu.VMEM)
    hbm = pl.BlockSpec(memory_space=pltpu.HBM)
    mixed, loss, counts = pl.pallas_call(
        kernel,
        name="moe",
        out_shape=(
            jax.ShapeDtypeStruct((TOK, DH), BF16),
            jax.ShapeDtypeStruct((1, NB), F32),
            jax.ShapeDtypeStruct((1, NB), jnp.int32),
        ),
        in_specs=[hbm] * 9,
        out_specs=(hbm, vmem, vmem),
        scratch_shapes=[
            pltpu.VMEM((TOK, DH), BF16),
            pltpu.VMEM((TOK, DH), BF16),
            pltpu.VMEM((NE, DH), BF16),
            pltpu.VMEM((2, TOK), jnp.int32),
            pltpu.VMEM((1, NSEQ), jnp.int32),
            pltpu.VMEM((1, NSEQ), jnp.int32),
            pltpu.VMEM((TOK, DH), BF16),
            pltpu.VMEM((NE, CAP, DH), BF16),
            pltpu.VMEM((NE, CAP, DH), BF16),
            pltpu.VMEM((4, 2, 128, DH), BF16),
            pltpu.VMEM((4, 2, 128, DH), BF16),
            pltpu.VMEM((2, HID, DH), BF16),
            pltpu.VMEM((2, HID, DH), BF16),
            pltpu.VMEM((2, HID, DH), BF16),
            pltpu.VMEM((256, HID), BF16),
            pltpu.VMEM((4, 256, DH), BF16),
            pltpu.VMEM((4, 256, DH), BF16),
            pltpu.VMEM((4, 256, DH), F32),
            pltpu.VMEM((3, 2, 128, DH), BF16),
            pltpu.VMEM((2, 128, DH), BF16),
            pltpu.VMEM((2, 2, 128, DH), BF16),
            pltpu.VMEM((2, 128, DH), BF16),
            pltpu.VMEM((2, 32, DH), BF16),
            pltpu.VMEM((2, 2, 32, DH), BF16),
            pltpu.VMEM((NE, CAP, DH), BF16),
            pltpu.VMEM((NE, CAP, DH), BF16),
            pltpu.VMEM((TOK, 128), F32),
            pltpu.VMEM((TOK, 128), F32),
            pltpu.VMEM((16, 1, 128), F32),
            pltpu.VMEM((16, 1, 128), F32),
            pltpu.SemaphoreType.DMA((13,)),
            pltpu.SemaphoreType.DMA((NSEMS,)),
            pltpu.SemaphoreType.DMA((NSEMS,)),
        ],
        compiler_params=pltpu.CompilerParams(
            collective_id=0, has_side_effects=True, vmem_limit_bytes=66 * 1000 * 1000
        ),
    )(
        tokens, target, router.T, w_gate.swapaxes(1, 2), w_up.swapaxes(1, 2), w_down, expert_ids.T,
        lengths.reshape(1, NSEQ), bench_ids.reshape(1, NSEQ),
    )
    mixed, loss, counts = pl.pallas_call(
        hand_over,
        name="hand_over",
        out_shape=(
            jax.ShapeDtypeStruct((TOK, DH), BF16),
            jax.ShapeDtypeStruct((1, NB), F32),
            jax.ShapeDtypeStruct((1, NB), jnp.int32),
        ),
        in_specs=[hbm, hbm, hbm],
        out_specs=(hbm, hbm, hbm),
        scratch_shapes=[
            pltpu.VMEM((TOK, DH), BF16),
            pltpu.VMEM((1, NB), F32),
            pltpu.VMEM((1, NB), jnp.int32),
            pltpu.SemaphoreType.DMA((6,)),
        ],
        compiler_params=pltpu.CompilerParams(vmem_limit_bytes=66 * 1000 * 1000),
    )(mixed, loss, counts)
    return (mixed, loss.reshape(NB), counts.reshape(NB))


def solution(mesh):
    split = Mesh(
        mesh.devices.reshape(4, 4, mesh.shape["expert"], mesh.shape["tensor"]),
        ("dp_0", "dp_1", "expert", "tensor"),
    )
    in_specs = (
        P(DP_EXPERT, "tensor"),
        P(DP_EXPERT, "tensor"),
        P("tensor", None),
        P("expert", None, DP_TENSOR),
        P("expert", None, DP_TENSOR),
        P("expert", DP_TENSOR, None),
        P(DP_EXPERT, None),
        P(),
        P(),
    )
    out_specs = (P(DP_EXPERT, "tensor"), P(), P())
    return jax.shard_map(
        per_device, mesh=split, in_specs=in_specs, out_specs=out_specs, check_vma=False
    )
```

time: 104 us -> 85.8 us (0.82)
  Pallas kernels: 99.8 us -> 85.1 us
  local copies, waits for them, and re-layouts: 3.7 us -> 0 us
    pallas_call x1, Pallas kernels: 99.8 us -> 83.5 us  [per_device(): pl.pallas_call(kernel, name='moe', out_shape=(jax.ShapeDtypeStruct((TOK,...]
    unnamed x3 -> x0, local copies, waits for them, and re-layouts: 3.7 us -> none
    pallas_call x0 -> x1, Pallas kernels: none -> 1.53 us  [per_device(): pl.pallas_call(hand_over, name='hand_over', out_shape=(jax.ShapeDtypeStru...]
where the time goes in v2:
time: 85.8 us; the launch traced here: 85.7 us
  Pallas kernels  85.1 us (99%)
    pallas_call x1, Pallas kernels, per_device(): pl.pallas_call(kernel, name='moe', out_shape=(jax.ShapeDtypeStruct((TOK,...  83.5 us

profile of v2, /device:TPU:1, one launch (start us, length us, event | category | flops | bytes accessed | tf_op | source)
XLA Modules:
  0.0 85.7 jit_solution(1818330537479961643)
XLA Ops:
  0.6 83.5 %moe.1 = (bf16[16,2048]{1,0:T(8,128)(2,1)}, f32[1,16]{1,0:T(1,128)}, s32[1,16]{1,0:T(1,128)}) custom-call(bf16[16,2048]{1,0:T(8,128)(2,1)} %tokens_hbm.1, bf16[16,2048]{1,0:T(8,128)(2,1)} %target_hbm.1, bf16[8,2048]{1,0:T(8,128)(2,1)} %bitcast.10, bf16[1,448,4096]{2,1,0:T(8,128)(2,1)} %bitcast.8, bf16[1,448,4096]{2,1,0:T(8,128)(2,1)} %bitcast.9, ...), custom_call_target="tpu_custom_call" | custom-call | tf_op jit(solution)/shard_map/moe/pallas_call | solution.py:372
  84.2 1.5 %hand_over.1 = (bf16[16,2048]{1,0:T(8,128)(2,1)}, f32[1,16]{1,0:T(1,128)}, s32[1,16]{1,0:T(1,128)}) custom-call(bf16[16,2048]{1,0:T(8,128)(2,1)} %get-tuple-element.9.refs_0_, f32[1,16]{1,0:T(1,128)} %get-tuple-element.10.refs_1_, s32[1,16]{1,0:T(1,128)} %get-tuple-element.11.refs_2_), custom_call_target="tpu_custom_call" | custom-call | tf_op jit(solution)/shard_map/hand_over/pallas_call | solution.py:424

commit v3 on v2

--- a/solution.py
+++ b/solution.py
@@ -21,14 +21,14 @@
 MESH = pl.DeviceIdType.MESH
 F32 = jnp.float32
 BF16 = jnp.bfloat16
-NSEMS = 19 * NQ + 3
+NSEMS = 46
 
 
 def kernel(
     tokens_hbm, target_hbm, router_hbm, wg_hbm, wu_hbm, wd_hbm, ids_hbm, lengths_hbm, bench_hbm,
-    mixed_hbm, loss_out, counts_out,
-    tokens, target, router, ids, lengths, bench, mixed_out,
-    OUT, ZL, XO, XP, WG, WU, WD, H, PX, PR, PO, S, R1, R2, TB, T1, T2, RET, BACK,
+    mixed_out, loss_out, counts_out,
+    tokens, target, router, ids, lengths, bench,
+    OUT, ZL, ZR, XO, XP, WG, WU, WD, G, H, PX, PR, PO, S, R1, R2, TB, T1, T2, RET, BACK,
     LG, LGR, L1, L2, wsem, ssem, rsem,
 ):
     y = lax.axis_index("dp_0")
@@ -146,21 +146,32 @@
     def from_z(q, lanes):
         arrived(("z", q), ZL.at[1:8, :, lanes])
         for ab in range(2):
-            rows = ZL[4 * ab : 4 * ab + 4, :, lanes].astype(F32).reshape(32, FQ)
-            XO[0, ab, 0:32, lanes] = rows.astype(BF16)
-            src = XO.at[0, ab, 0:32, lanes]
-            send(("near_small", q), src, XO.at[0, ab, 96:128, lanes], small_axis(ab, 1))
-            send(("near_small", q), src, XO.at[0, ab, 32:64, lanes], small_axis(ab, 3))
+            rows = ZL[4 * ab : 4 * ab + 4, :, lanes].astype(F32).reshape(32, FQ).astype(BF16)
+            ZR[ab, :, lanes] = rows
+            XO[0, ab, 0:16, lanes] = rows[0:16]
+            XO[0, ab, 112:128, lanes] = rows[16:32]
+        for ab in range(2):
+            src = ZR.at[ab, :, lanes]
+            send(("near_small", q), src, XO.at[0, ab, 80:112, lanes], small_axis(ab, 1))
+            send(("near_small", q), src, XO.at[0, ab, 16:48, lanes], small_axis(ab, 3))
+        for ab in range(2):
+            early(q, lanes, ab, 0, 16)
+
+    def early(q, lanes, ab, start, stop):
+        for rows, step in ((slice(start, stop), 1), (slice(128 - stop, 128 - start), 3)):
+            send(("near", q), XO.at[0, ab, rows, lanes], XO.at[1, ab, rows, lanes], large_axis(ab, step))
 
     def small_forward(q, lanes):
         arrived(("near_small", q), XO.at[0, :, 0:64, lanes])
         for ab in range(2):
             send(
-                ("far_small", q), XO.at[0, ab, 96:112, lanes], XO.at[0, ab, 64:80, lanes], small_axis(ab, 1)
+                ("far_small", q), XO.at[0, ab, 80:96, lanes], XO.at[0, ab, 48:64, lanes], small_axis(ab, 1)
             )
             send(
-                ("far_small", q), XO.at[0, ab, 48:64, lanes], XO.at[0, ab, 80:96, lanes], small_axis(ab, 3)
+                ("far_small", q), XO.at[0, ab, 32:48, lanes], XO.at[0, ab, 64:80, lanes], small_axis(ab, 3)
             )
+        for ab in range(2):
+            early(q, lanes, ab, 16, 48)
 
     def to_partner(unit, q, lanes):
         send(("across", unit, q), XO.at[unit, :, :, lanes], XP.at[unit, :, :, lanes], at(dc=1))
@@ -168,10 +179,10 @@
     def large_own(q, lanes):
         arrived(("far_small", q), XO.at[0, :, 0:32, lanes])
         for ab in range(2):
-            upper, lower = XO.at[0, ab, 0:64, lanes], XO.at[0, ab, 64:128, lanes]
-            send(("near", q), upper, XO.at[1, ab, 0:64, lanes], large_axis(ab, 1))
-            send(("near", q), lower, XO.at[1, ab, 64:128, lanes], large_axis(ab, 3))
+            early(q, lanes, ab, 48, 64)
         to_partner(0, q, lanes)
+        if q == 0:
+            late(0, lanes, 0, 32)
 
     def large_forward(q, lanes):
         arrived(("near", q), XO.at[1, :, :, lanes])
@@ -180,30 +191,35 @@
             send(("far", q), XO.at[1, ab, 64:128, lanes], XO.at[2, ab, 64:128, lanes], large_axis(ab, 3))
         to_partner(1, q, lanes)
 
+    def late(q, lanes, lower, upper):
+        for ab in range(2):
+            for rows, step in ((slice(128 - upper, 128 - lower), 1), (slice(lower, upper), 3)):
+                send(("late", q), XO.at[0, ab, rows, lanes], XO.at[3, ab, rows, lanes], large_axis(ab, step))
+
     wavefront((from_z, small_forward, large_own), (0, 1, 2))
     halves = [(q, pl.ds(q * FQ, FQ)) for q in range(NQ)]
-    large_forward(*halves[0])
-
-    for load in loads:
-        load.wait()
-
-    def up(unit):
+
+    def up_own(unit):
+        own = XO[unit].reshape(256, DH)
+        G[0] = lax.dot_general(WG[0], own, by_rows, preferred_element_type=F32)
+        G[1] = lax.dot_general(WU[0], own, by_rows, preferred_element_type=F32)
+
+    def up_other(unit):
         for q, lanes in halves:
             arrived(("across", unit, q), XP.at[unit, :, :, lanes])
-        own = XO[unit].reshape(256, DH)
         other = XP[unit].reshape(256, DH)
-        gate = lax.dot_general(WG[0], own, by_rows, preferred_element_type=F32)
-        gate += lax.dot_general(WG[1], other, by_rows, preferred_element_type=F32)
-        raise_ = lax.dot_general(WU[0], own, by_rows, preferred_element_type=F32)
-        raise_ += lax.dot_general(WU[1], other, by_rows, preferred_element_type=F32)
+        gate = G[0] + lax.dot_general(WG[1], other, by_rows, preferred_element_type=F32)
+        raise_ = G[1] + lax.dot_general(WU[1], other, by_rows, preferred_element_type=F32)
         H[...] = (gate * jax.nn.sigmoid(gate) * raise_).astype(BF16).T
 
-    def down(unit):
+    def down(unit, between=None):
         for q, lanes in halves:
             for n in range(q * FQ, q * FQ + FQ, 512):
                 cols = slice(n, n + 512)
                 PX[unit, :, cols] = jnp.dot(H[...], WD[1, :, cols], preferred_element_type=F32).astype(BF16)
             send(("sums", unit, q), PX.at[unit, :, lanes], PR.at[unit, :, lanes], at(dc=1))
+        if between is not None:
+            between()
         for n in range(0, DH, 512):
             cols = slice(n, n + 512)
             PO[unit, :, cols] = jnp.dot(H[...], WD[0, :, cols], preferred_element_type=F32)
@@ -212,35 +228,43 @@
         arrived(("sums", unit, q), PR.at[unit, :, lanes])
         return PO[unit, :, lanes] + PR[unit, :, lanes].astype(F32)
 
-    up(0)
+    for load in loads:
+        load.wait()
+    up_own(0)
+    large_forward(*halves[0])
+    up_other(0)
     large_forward(*halves[1])
-    for q, lanes in halves:
-        for ab in range(2):
-            upper, lower = XO.at[0, ab, 0:64, lanes], XO.at[0, ab, 64:128, lanes]
-            send(("late", q), lower, XO.at[3, ab, 64:128, lanes], large_axis(ab, 1))
-            send(("late", q), upper, XO.at[3, ab, 0:64, lanes], large_axis(ab, 3))
+    late(*halves[0], 32, 64)
+    late(*halves[1], 0, 64)
     down(0)
-    up(1)
+    up_own(1)
+    up_other(1)
     down(1)
     for q, lanes in halves:
         arrived(("far", q), XO.at[2, :, :, lanes])
         to_partner(2, q, lanes)
+    up_own(2)
     for q, lanes in halves:
         S[0, :, :, lanes] = chip_sum(1, q, lanes).astype(BF16).reshape(2, 128, FQ)
         for ab in range(2):
-            send(("sent", q), S.at[0, ab, 64:128, lanes], R2.at[0, ab, 64:128, lanes], large_axis(ab, 1))
-            send(("sent", q), S.at[0, ab, 0:64, lanes], R2.at[1, ab, 0:64, lanes], large_axis(ab, 3))
-    up(2)
-    for q, lanes in halves:
-        arrived(("late", q), XO.at[3, :, :, lanes])
-        to_partner(3, q, lanes)
-    down(2)
+            send("direct", S.at[0, ab, 64:128, lanes], R2.at[0, ab, 64:128, lanes], large_axis(ab, 1))
+            send("direct", S.at[0, ab, 0:64, lanes], R2.at[1, ab, 0:64, lanes], large_axis(ab, 3))
+    up_other(2)
+    def last_block():
+        for q, lanes in halves:
+            arrived(("late", q), XO.at[3, :, :, lanes])
+            to_partner(3, q, lanes)
+
+    down(2, last_block)
+    up_own(3)
+    parts_of = ((48, 64), (16, 48), (0, 16))
     for q, lanes in halves:
         S[1, :, :, lanes] = chip_sum(2, q, lanes).astype(BF16).reshape(2, 128, FQ)
-        for ab in range(2):
-            send(("first", q), S.at[1, ab, 0:64, lanes], R1.at[ab, 0:64, lanes], large_axis(ab, 1))
-            send(("first", q), S.at[1, ab, 64:128, lanes], R1.at[ab, 64:128, lanes], large_axis(ab, 3))
-    up(3)
+    for part, (start, stop) in enumerate(parts_of):
+        for ab in range(2):
+            for rows, step in ((slice(start, stop), 1), (slice(128 - stop, 128 - start), 3)):
+                send(("first", part), S.at[1, ab, rows], R1.at[ab, rows], large_axis(ab, step))
+    up_other(3)
     down(3)
     arrived("logits", LGR)
     logits = LG[...] + LGR[...]
@@ -274,48 +298,70 @@
     counts = lax.dot_general(less_one, table, by_rows, preferred_element_type=F32)[0:1]
 
     for q, lanes in halves:
-        total = chip_sum(3, q, lanes)
-        arrived(("first", q), R1.at[:, :, lanes])
-        S[2, :, :, lanes] = (total.reshape(2, 128, FQ) + R1[:, :, lanes].astype(F32)).astype(BF16)
-        for ab in range(2):
-            send(("sent", q), S.at[2, ab, 0:64, lanes], R2.at[0, ab, 0:64, lanes], large_axis(ab, 1))
-            send(("sent", q), S.at[2, ab, 64:128, lanes], R2.at[1, ab, 64:128, lanes], large_axis(ab, 3))
-    for q, lanes in halves:
         PO[0, :, lanes] = chip_sum(0, q, lanes)
+    for q, lanes in halves:
+        PO[3, :, lanes] = chip_sum(3, q, lanes)
+    def second(part):
+        start, stop = parts_of[part]
+        arrived(("first", part), R1.at[:, 0 : 2 * (stop - start)])
+        for ab in range(2):
+            for slot, rows, step in ((0, slice(start, stop), 1), (1, slice(128 - stop, 128 - start), 3)):
+                mine = slice(128 * ab + rows.start, 128 * ab + rows.stop)
+                S[2, ab, rows] = (PO[3, mine] + R1[ab, rows].astype(F32)).astype(BF16)
+                send(("second", part), S.at[2, ab, rows], R2.at[slot, ab, rows], large_axis(ab, step))
+
+    second(0)
+    second(1)
+    arrived("direct", R1)
+
+    def total_of(ab, rows):
+        mine = slice(128 * ab + rows.start, 128 * ab + rows.stop)
+        total = PO[0, mine] + R2[0, ab, rows].astype(F32)
+        return mine, total + R2[1, ab, rows].astype(F32)
+
+    arrived(("second", 0), R1.at[:, 0:32])
+    for ab in range(2):
+        for rows, to, step in ((slice(48, 64), slice(0, 16), 1), (slice(64, 80), slice(16, 32), 3)):
+            TB[ab, rows] = total_of(ab, rows)[1].astype(BF16)
+            send("first_small", TB.at[ab, rows], T1.at[ab, to], small_axis(ab, step))
+    second(2)
+    arrived(("second", 1), R1.at[:, 0:64])
+    for ab in range(2):
+        for rows, to, slot, step in (
+            (slice(32, 48), slice(16, 32), 0, 1),
+            (slice(80, 96), slice(0, 16), 1, 3),
+        ):
+            TB[ab, rows] = total_of(ab, rows)[1].astype(BF16)
+            send("direct_small", TB.at[ab, rows], T2.at[slot, ab, to], small_axis(ab, step))
+        for rows in (slice(16, 32), slice(96, 112)):
+            mine, total = total_of(ab, rows)
+            PO[0, mine] = total
+    arrived("first_small", T1)
+    for q, lanes in halves:
+        for ab in range(2):
+            for rows, half, slot, step in (
+                (slice(16, 32), slice(0, 16), 0, 1),
+                (slice(96, 112), slice(16, 32), 1, 3),
+            ):
+                mine = slice(128 * ab + rows.start, 128 * ab + rows.stop)
+                TB[ab, rows, lanes] = (PO[0, mine, lanes] + T1[ab, half, lanes].astype(F32)).astype(BF16)
+                send(("sent_small", q), TB.at[ab, rows, lanes], T2.at[slot, ab, half, lanes], small_axis(ab, step))
+    arrived(("second", 2), R1.at[:, 0:32])
+    for ab in range(2):
+        for rows in (slice(0, 16), slice(112, 128)):
+            mine, total = total_of(ab, rows)
+            PO[0, mine] = total
+    arrived("direct_small", T1)
     token_sums = []
 
-    def large_total(q, lanes):
-        arrived(("sent", q), R2.at[:, :, :, lanes])
-        for ab in range(2):
-            block = slice(128 * ab, 128 * ab + 128)
-            total = PO[0, block, lanes] + R2[0, ab, :, lanes].astype(F32)
-            total += R2[1, ab, :, lanes].astype(F32)
-            PO[0, block, lanes] = total
-            TB[ab, :, lanes] = total.astype(BF16)
-            send(("first_small", q), TB.at[ab, 64:80, lanes], T1.at[ab, 0:16, lanes], small_axis(ab, 1))
-            send(("first_small", q), TB.at[ab, 80:96, lanes], T1.at[ab, 16:32, lanes], small_axis(ab, 3))
-            send(("sent_small", q), TB.at[ab, 48:64, lanes], T2.at[0, ab, 16:32, lanes], small_axis(ab, 1))
-            send(("sent_small", q), TB.at[ab, 96:112, lanes], T2.at[1, ab, 0:16, lanes], small_axis(ab, 3))
-
-    def small_step(q, lanes):
-        arrived(("first_small", q), T1.at[:, :, lanes])
-        for ab in range(2):
-            for rel, base, half, slot in ((1, 32, slice(0, 16), 0), (3, 96, slice(16, 32), 1)):
-                rows = slice(base + half.start, base + half.stop)
-                TB[ab, rows, lanes] = (
-                    PO[0, 128 * ab + rows.start : 128 * ab + rows.stop, lanes] + T1[ab, half, lanes].astype(F32)
-                ).astype(BF16)
-                send(
-                    ("sent_small", q), TB.at[ab, rows, lanes], T2.at[slot, ab, half, lanes], small_axis(ab, rel)
-                )
-
     def small_total(q, lanes):
-        arrived(("sent_small", q), T2.at[:, :, :, lanes])
-        for ab in range(2):
-            total = PO[0, 128 * ab : 128 * ab + 32, lanes]
-            total += T2[0, ab, :, lanes].astype(F32)
-            total += T2[1, ab, :, lanes].astype(F32)
-            RET[4 * ab : 4 * ab + 4, :, lanes] = total.reshape(4, CAP, FQ).astype(BF16)
+        arrived(("sent_small", q), T1.at[:, :, lanes])
+        for ab in range(2):
+            for top, half, first_z in ((0, slice(0, 16), 4 * ab), (112, slice(16, 32), 4 * ab + 2)):
+                total = PO[0, 128 * ab + top : 128 * ab + top + 16, lanes]
+                total += T2[0, ab, half, lanes].astype(F32)
+                total += T2[1, ab, half, lanes].astype(F32)
+                RET[first_z : first_z + 2, :, lanes] = total.reshape(2, CAP, FQ).astype(BF16)
         BACK[0, :, lanes] = RET[0, :, lanes]
         for j in (4, 3, 5, 2, 6, 1, 7):
             send(("back", q), RET.at[j, :, lanes], BACK.at[8 - j, :, lanes], at(dz=j))
@@ -329,12 +375,10 @@
         diff = mixed.astype(F32) - target[:, lanes].astype(F32)
         token_sums.append(jnp.sum(diff * diff, axis=1, keepdims=True))
 
-    wavefront((large_total, small_step, small_total, mix), (0, 1, 2, 4))
+    wavefront((small_total, mix), (0, 2))
     token_sum = sum(token_sums[1:], token_sums[0])
     sums = jnp.sum(bench_of * (token_sum / D), axis=0, keepdims=True)
 
-    hand = pltpu.make_async_copy(mixed_out, mixed_hbm, wsem.at[12])
-    hand.start()
     mine = z * 2 + c
     L1[mine] = sums
     for dz, dc in column:
@@ -348,21 +392,16 @@
     loss_sum = jnp.sum(L2[...], axis=0)
     loss_out[...] = (loss_sum / jnp.maximum(counts, 1.0))[:, 0:NB]
     counts_out[...] = counts[:, 0:NB].astype(jnp.int32)
-    hand.wait()
     for copy in waits:
         copy.wait_send()
 
 
 def hand_over(*refs):
-    sources, targets, stages, sems = refs[0:3], refs[3:6], refs[6:9], refs[9]
-    arriving = [pltpu.make_async_copy(sources[i], stages[i], sems.at[i]) for i in range(3)]
-    leaving = [pltpu.make_async_copy(stages[i], targets[i], sems.at[3 + i]) for i in range(3)]
-    for copy in arriving:
+    sources, targets, sems = refs[0:3], refs[3:6], refs[6]
+    copies = [pltpu.make_async_copy(sources[i], targets[i], sems.at[i]) for i in range(3)]
+    for copy in copies:
         copy.start()
-    for i in range(3):
-        arriving[i].wait()
-        leaving[i].start()
-    for copy in leaving:
+    for copy in copies:
         copy.wait()
 
 
@@ -373,12 +412,12 @@
         kernel,
         name="moe",
         out_shape=(
-            jax.ShapeDtypeStruct((TOK, DH), BF16),
-            jax.ShapeDtypeStruct((1, NB), F32),
-            jax.ShapeDtypeStruct((1, NB), jnp.int32),
+            pltpu.VMEM((TOK, DH), BF16),
+            pltpu.VMEM((1, NB), F32),
+            pltpu.VMEM((1, NB), jnp.int32),
         ),
         in_specs=[hbm] * 9,
-        out_specs=(hbm, vmem, vmem),
+        out_specs=(vmem, vmem, vmem),
         scratch_shapes=[
             pltpu.VMEM((TOK, DH), BF16),
             pltpu.VMEM((TOK, DH), BF16),
@@ -386,14 +425,15 @@
             pltpu.VMEM((2, TOK), jnp.int32),
             pltpu.VMEM((1, NSEQ), jnp.int32),
             pltpu.VMEM((1, NSEQ), jnp.int32),
-            pltpu.VMEM((TOK, DH), BF16),
             pltpu.VMEM((NE, CAP, DH), BF16),
             pltpu.VMEM((NE, CAP, DH), BF16),
+            pltpu.VMEM((2, 32, DH), BF16),
             pltpu.VMEM((4, 2, 128, DH), BF16),
             pltpu.VMEM((4, 2, 128, DH), BF16),
             pltpu.VMEM((2, HID, DH), BF16),
             pltpu.VMEM((2, HID, DH), BF16),
             pltpu.VMEM((2, HID, DH), BF16),
+            pltpu.VMEM((2, HID, 256), F32),
             pltpu.VMEM((256, HID), BF16),
             pltpu.VMEM((4, 256, DH), BF16),
             pltpu.VMEM((4, 256, DH), BF16),
@@ -410,7 +450,7 @@
             pltpu.VMEM((TOK, 128), F32),
             pltpu.VMEM((16, 1, 128), F32),
             pltpu.VMEM((16, 1, 128), F32),
-            pltpu.SemaphoreType.DMA((13,)),
+            pltpu.SemaphoreType.DMA((12,)),
             pltpu.SemaphoreType.DMA((NSEMS,)),
             pltpu.SemaphoreType.DMA((NSEMS,)),
         ],
@@ -429,15 +469,10 @@
             jax.ShapeDtypeStruct((1, NB), F32),
             jax.ShapeDtypeStruct((1, NB), jnp.int32),
         ),
-        in_specs=[hbm, hbm, hbm],
+        in_specs=[vmem, vmem, vmem],
         out_specs=(hbm, hbm, hbm),
-        scratch_shapes=[
-            pltpu.VMEM((TOK, DH), BF16),
-            pltpu.VMEM((1, NB), F32),
-            pltpu.VMEM((1, NB), jnp.int32),
-            pltpu.SemaphoreType.DMA((6,)),
-        ],
-        compiler_params=pltpu.CompilerParams(vmem_limit_bytes=66 * 1000 * 1000),
+        scratch_shapes=[pltpu.SemaphoreType.DMA((3,))],
+        compiler_params=pltpu.CompilerParams(vmem_limit_bytes=4 * 1024 * 1024),
     )(mixed, loss, counts)
     return (mixed, loss.reshape(NB), counts.reshape(NB))
 

time: 85.8 us -> 79.7 us (0.929)
  Pallas kernels: 85.1 us -> 79 us
    pallas_call x1, Pallas kernels: 83.5 us -> 78.3 us  [per_device(): pl.pallas_call(kernel, name='moe', out_shape=(pltpu.VMEM((TOK, DH), BF16)...]
    pallas_call x1, Pallas kernels: 1.53 us -> 0.66 us  [per_device(): pl.pallas_call(hand_over, name='hand_over', out_shape=(jax.ShapeDtypeStru...]
where the time goes in v3:
time: 79.7 us
  Pallas kernels  79 us (99%)
    pallas_call x1, Pallas kernels, per_device(): pl.pallas_call(kernel, name='moe', out_shape=(pltpu.VMEM((TOK, DH), BF16)...  78.3 us

profile of v3, /device:TPU:1, one launch (start us, length us, event | category | flops | bytes accessed | tf_op | source)
XLA Modules:
  0.0 79.7 jit_solution(2703888950598040012)
XLA Ops:
  0.6 78.3 %moe.1 = (bf16[16,2048]{1,0:T(8,128)(2,1)S(1)}, f32[1,16]{1,0:T(1,128)S(1)}, s32[1,16]{1,0:T(1,128)S(1)}) custom-call(bf16[16,2048]{1,0:T(8,128)(2,1)} %tokens_hbm.1, bf16[16,2048]{1,0:T(8,128)(2,1)} %target_hbm.1, bf16[8,2048]{1,0:T(8,128)(2,1)} %bitcast.10, bf16[1,448,4096]{2,1,0:T(8,128)(2,1)} %bitcast.8, bf16[1,448,4096]{2,1,0:T(8,128)(2,1)} %bitcast.9, ...), custom_call_target="tpu_custom_call" | custom-call | tf_op jit(solution)/shard_map/moe/pallas_call | solution.py:411
  79.0 0.7 hand_over.1

commit v4 on v3

--- a/solution.py
+++ b/solution.py
@@ -21,7 +21,7 @@
 MESH = pl.DeviceIdType.MESH
 F32 = jnp.float32
 BF16 = jnp.bfloat16
-NSEMS = 46
+NSEMS = 48
 
 
 def kernel(
@@ -152,8 +152,8 @@
             XO[0, ab, 112:128, lanes] = rows[16:32]
         for ab in range(2):
             src = ZR.at[ab, :, lanes]
-            send(("near_small", q), src, XO.at[0, ab, 80:112, lanes], small_axis(ab, 1))
-            send(("near_small", q), src, XO.at[0, ab, 16:48, lanes], small_axis(ab, 3))
+            send(("near_small", q, ab), src, XO.at[0, ab, 80:112, lanes], small_axis(ab, 1))
+            send(("near_small", q, ab), src, XO.at[0, ab, 16:48, lanes], small_axis(ab, 3))
         for ab in range(2):
             early(q, lanes, ab, 0, 16)
 
@@ -162,13 +162,13 @@
             send(("near", q), XO.at[0, ab, rows, lanes], XO.at[1, ab, rows, lanes], large_axis(ab, step))
 
     def small_forward(q, lanes):
-        arrived(("near_small", q), XO.at[0, :, 0:64, lanes])
-        for ab in range(2):
+        for ab in range(2):
+            arrived(("near_small", q, ab), XO.at[0, ab, 0:64, lanes])
             send(
-                ("far_small", q), XO.at[0, ab, 80:96, lanes], XO.at[0, ab, 48:64, lanes], small_axis(ab, 1)
+                ("far_small", q, ab), XO.at[0, ab, 80:96, lanes], XO.at[0, ab, 48:64, lanes], small_axis(ab, 1)
             )
             send(
-                ("far_small", q), XO.at[0, ab, 32:48, lanes], XO.at[0, ab, 64:80, lanes], small_axis(ab, 3)
+                ("far_small", q, ab), XO.at[0, ab, 32:48, lanes], XO.at[0, ab, 64:80, lanes], small_axis(ab, 3)
             )
         for ab in range(2):
             early(q, lanes, ab, 16, 48)
@@ -177,8 +177,8 @@
         send(("across", unit, q), XO.at[unit, :, :, lanes], XP.at[unit, :, :, lanes], at(dc=1))
 
     def large_own(q, lanes):
-        arrived(("far_small", q), XO.at[0, :, 0:32, lanes])
-        for ab in range(2):
+        for ab in range(2):
+            arrived(("far_small", q, ab), XO.at[0, ab, 0:32, lanes])
             early(q, lanes, ab, 48, 64)
         to_partner(0, q, lanes)
         if q == 0:
@@ -231,41 +231,6 @@
     for load in loads:
         load.wait()
     up_own(0)
-    large_forward(*halves[0])
-    up_other(0)
-    large_forward(*halves[1])
-    late(*halves[0], 32, 64)
-    late(*halves[1], 0, 64)
-    down(0)
-    up_own(1)
-    up_other(1)
-    down(1)
-    for q, lanes in halves:
-        arrived(("far", q), XO.at[2, :, :, lanes])
-        to_partner(2, q, lanes)
-    up_own(2)
-    for q, lanes in halves:
-        S[0, :, :, lanes] = chip_sum(1, q, lanes).astype(BF16).reshape(2, 128, FQ)
-        for ab in range(2):
-            send("direct", S.at[0, ab, 64:128, lanes], R2.at[0, ab, 64:128, lanes], large_axis(ab, 1))
-            send("direct", S.at[0, ab, 0:64, lanes], R2.at[1, ab, 0:64, lanes], large_axis(ab, 3))
-    up_other(2)
-    def last_block():
-        for q, lanes in halves:
-            arrived(("late", q), XO.at[3, :, :, lanes])
-            to_partner(3, q, lanes)
-
-    down(2, last_block)
-    up_own(3)
-    parts_of = ((48, 64), (16, 48), (0, 16))
-    for q, lanes in halves:
-        S[1, :, :, lanes] = chip_sum(2, q, lanes).astype(BF16).reshape(2, 128, FQ)
-    for part, (start, stop) in enumerate(parts_of):
-        for ab in range(2):
-            for rows, step in ((slice(start, stop), 1), (slice(128 - stop, 128 - start), 3)):
-                send(("first", part), S.at[1, ab, rows], R1.at[ab, rows], large_axis(ab, step))
-    up_other(3)
-    down(3)
     arrived("logits", LGR)
     logits = LG[...] + LGR[...]
     picked_0 = jnp.sum(logits * marks_0, axis=1, keepdims=True)
@@ -297,6 +262,41 @@
     less_one = jnp.broadcast_to(counted - 1.0, (8, NSEQ)).astype(BF16)
     counts = lax.dot_general(less_one, table, by_rows, preferred_element_type=F32)[0:1]
 
+    large_forward(*halves[0])
+    up_other(0)
+    large_forward(*halves[1])
+    late(*halves[0], 32, 64)
+    late(*halves[1], 0, 64)
+    down(0)
+    up_own(1)
+    up_other(1)
+    down(1)
+    for q, lanes in halves:
+        arrived(("far", q), XO.at[2, :, :, lanes])
+        to_partner(2, q, lanes)
+    up_own(2)
+    for q, lanes in halves:
+        S[0, :, :, lanes] = chip_sum(1, q, lanes).astype(BF16).reshape(2, 128, FQ)
+    for ab in range(2):
+        send("direct", S.at[0, ab, 64:128], R2.at[0, ab, 64:128], large_axis(ab, 1))
+        send("direct", S.at[0, ab, 0:64], R2.at[1, ab, 0:64], large_axis(ab, 3))
+    up_other(2)
+    def last_block():
+        for q, lanes in halves:
+            arrived(("late", q), XO.at[3, :, :, lanes])
+            to_partner(3, q, lanes)
+
+    down(2, last_block)
+    up_own(3)
+    parts_of = ((48, 64), (16, 48), (0, 16))
+    for q, lanes in halves:
+        S[1, :, :, lanes] = chip_sum(2, q, lanes).astype(BF16).reshape(2, 128, FQ)
+    for part, (start, stop) in enumerate(parts_of):
+        for ab in range(2):
+            for rows, step in ((slice(start, stop), 1), (slice(128 - stop, 128 - start), 3)):
+                send(("first", part), S.at[1, ab, rows], R1.at[ab, rows], large_axis(ab, step))
+    up_other(3)
+    down(3)
     for q, lanes in halves:
         PO[0, :, lanes] = chip_sum(0, q, lanes)
     for q, lanes in halves:

time: 79.7 us -> 80.1 us (level)
  no operation moved by 1% of the time
where the time goes in v4:
time: 80.1 us; the launch traced here: 80 us
  Pallas kernels  79.4 us (99%)
    pallas_call x1, Pallas kernels, per_device(): pl.pallas_call(kernel, name='moe', out_shape=(pltpu.VMEM((TOK, DH), BF16)...  78.7 us

profile of v4, /device:TPU:1, one launch (start us, length us, event | category | flops | bytes accessed | tf_op | source)
XLA Modules:
  0.0 80.0 jit_solution(16972607965237627878)
XLA Ops:
  0.6 78.7 %moe.1 = (bf16[16,2048]{1,0:T(8,128)(2,1)S(1)}, f32[1,16]{1,0:T(1,128)S(1)}, s32[1,16]{1,0:T(1,128)S(1)}) custom-call(bf16[16,2048]{1,0:T(8,128)(2,1)} %tokens_hbm.1, bf16[16,2048]{1,0:T(8,128)(2,1)} %target_hbm.1, bf16[8,2048]{1,0:T(8,128)(2,1)} %bitcast.10, bf16[1,448,4096]{2,1,0:T(8,128)(2,1)} %bitcast.8, bf16[1,448,4096]{2,1,0:T(8,128)(2,1)} %bitcast.9, ...), custom_call_target="tpu_custom_call" | custom-call | tf_op jit(solution)/shard_map/moe/pallas_call | solution.py:411
  79.4 0.7 hand_over.1
